TPU v7x, 256 devices: a whole 4x4x8 slice. The times are simulated.
256 devices in a mesh: row: 32 (over x, z), col: 8 (over y, core).
Axes of the slice: x: 4, y: 4, z: 8, core: 2. Of those that a mesh axis runs over, the one named last changes fastest.
Arguments:
- matrix: float32 [5, 32, 20, 8, 128, 128], P(None, 'row', None, 'col'), may hold values from 0 to 2.5, as said below
- flags: int32 [5, 32, 20, 8], P(None, 'row', None, 'col'), may hold values from 0 to 1, as said below
Outputs:
- factor: float32 [5, 32, 20, 8, 128, 128], P(None, 'row', None, 'col')
Inputs may be any that keep to these rules, and one draw needn't show every extreme that they name: `matrix`: symmetric positive definite, of order 160*128, diagonal at least 1.5. `flags`: 0 marks a float32 tile, 1 a bfloat16 tile; every diagonal tile is 0.
All inputs are finite; a program needn't handle non-finite values.
Results may differ from a plain program's by a relative error of at most 0.0005.
The roundings to bfloat16 on the way count: a program that leaves them out, or rounds other values in their place, can miss the bound.
Values sent between devices are 32-bit elements; how exact they have to be, the bound alone decides.
A program may use at most 128 MiB of HBM per device.

v0:
```python
import jax
import jax.numpy as jnp
from jax import lax
from jax.sharding import Mesh
from jax.sharding import PartitionSpec as P

PT = 4
ROW = ("row_0", "row_1")


def picked(shard, axis, root):
    return lax.dynamic_index_in_dim(lax.all_gather(shard, axis), root, 0, keepdims=False)


def spread(value, axis, source):
    kept = jnp.where(lax.axis_index(axis) == source, value, 0).astype(value.dtype)
    return lax.psum(kept, axis)


def from_root(shard, axes, root):
    shard = jnp.where(lax.axis_index(axes) == root, shard, jnp.zeros_like(shard))
    for axis in axes:
        shard = lax.psum(shard, axis)
    return shard


def storage_round(values):
    narrow = lax.optimization_barrier(values.astype(jnp.bfloat16))
    return narrow.astype(jnp.float32)


def solve_rows(lower_block, rows):
    width = rows.shape[2]
    flat = rows.reshape(-1, width)
    solved = jax.scipy.linalg.solve_triangular(lower_block, flat.T, lower=True).T
    return solved.reshape(rows.shape)


def with_block(solved, lower_block, global_ids, start):
    offset = jnp.clip(global_ids - start, 0, PT - 1)
    block_rows = lower_block.reshape(PT, solved.shape[1], solved.shape[2])[offset]
    inside = (global_ids >= start) & (global_ids < start + PT)
    return jnp.where(inside[:, None, None], block_rows, solved)


def factor_panel(work, start, row_ids, row_count, col_count):
    pieces = []
    for column in range(start, start + PT):
        pieces.append(picked(work[:, column // col_count], "col", column % col_count))
    panel_rows = jnp.concatenate(pieces, axis=2)
    blocks = []
    for tile_row in range(start, start + PT):
        blocks.append(spread(panel_rows[tile_row // row_count], ROW, tile_row % row_count))
    dense = jnp.concatenate(blocks, axis=0)
    sym = jnp.tril(dense) + jnp.tril(dense, -1).T
    lower_block = jnp.linalg.cholesky(sym)
    solved = with_block(solve_rows(lower_block, panel_rows), lower_block, row_ids, start)
    return (panel_rows, lower_block, solved)


def apply_update(work, marks, left, right, row_ids, col_ids, low, high):
    exact = jnp.einsum("aik,cjk->acij", left, right, precision=lax.Precision.HIGHEST)
    coarse = jnp.einsum(
        "aik,cjk->acij",
        left.astype(jnp.bfloat16),
        right.astype(jnp.bfloat16),
        preferred_element_type=jnp.float32,
    )
    live = (
        (row_ids[:, None] >= col_ids[None, :])
        & (col_ids >= low)[None, :]
        & (col_ids < high)[None, :]
    )
    updated = jnp.where((marks == 1)[:, :, None, None], work - coarse, work - exact)
    return jnp.where(live[:, :, None, None], updated, work)


def store_panel(work, solved, start, row_ids, col_index, col_count):
    tile = work.shape[2]
    for column in range(start, start + PT):
        slot = column // col_count
        offset = column - start
        piece = solved[:, :, offset * tile : (offset + 1) * tile]
        keep = (row_ids >= start)[:, None, None] & (col_index == column % col_count)
        work = work.at[:, slot].set(jnp.where(keep, piece, work[:, slot]))
    return work


def on_device(matrix, flags):
    row_count = lax.axis_size(ROW)
    col_count = lax.axis_size("col")
    row_index = lax.axis_index(ROW)
    col_index = lax.axis_index("col")
    tile_rows = matrix.shape[0]
    tile_cols = matrix.shape[2]
    tile = matrix.shape[4]
    tiles = matrix.reshape(tile_rows, tile_cols, tile, tile)
    marks = flags.reshape(tile_rows, tile_cols)
    row_ids = jnp.arange(tile_rows, dtype=jnp.int32) * row_count + row_index
    col_ids = jnp.arange(tile_cols, dtype=jnp.int32) * col_count + col_index
    work = jnp.where((marks == 1)[:, :, None, None], storage_round(tiles), tiles)
    beyond = 1 << 30
    lefts = []
    rights = []
    for step in range(2):
        start = step * PT
        panel_rows, lower_block, solved = factor_panel(work, start, row_ids, row_count, col_count)
        received = []
        for slot in range(tile_cols):
            column = col_ids[slot]
            piece = lax.dynamic_index_in_dim(panel_rows, column // row_count, 0, keepdims=False)
            received.append(from_root(piece, ROW, column % row_count))
        stacked = jnp.stack(received, axis=0)
        right = with_block(solve_rows(lower_block, stacked), lower_block, col_ids, start)
        lefts.append(solved)
        rights.append(right)
        work = apply_update(work, marks, solved, right, row_ids, col_ids, start + PT, beyond)
        work = store_panel(work, solved, start, row_ids, col_index, col_count)
    final = jnp.where((marks == 1)[:, :, None, None], storage_round(work), work)
    upper = row_ids[:, None] < col_ids[None, :]
    final = jnp.where(upper[:, :, None, None], jnp.float32(0.0), final)
    return final.reshape(matrix.shape)


def solution(mesh):
    finer = Mesh(mesh.devices.reshape(4, 8, mesh.shape["col"]), ("row_0", "row_1", "col"))
    in_specs = (P(None, ROW, None, "col", None, None), P(None, ROW, None, "col"))
    out_specs = P(None, ROW, None, "col", None, None)
    return jax.shard_map(
        on_device, mesh=finer, in_specs=in_specs, out_specs=out_specs, check_vma=False
    )
```

profile of v0, /device:TPU:32, one launch (start us, length us, event | category | flops | bytes accessed | tf_op | source)
XLA Modules:
  0.0 1065.8 jit_solution(9014248538773409077)
XLA Ops:
  7.3 8.1 copy.99
  15.5 3.7 bitcast_convert_fusion
  20.8 2.8 copy-done.1
  53.0 2.9 all-gather.5.cloned.1.call-done
  86.4 124.2 %all-reduce.16.cloned.1.call-done = (f32[128,512]{1,0:T(8,128)}, f32[128,512]{1,0:T(8,128)}, f32[128,512]{1,0:T(8,128)}, f32[128,512]{1,0:T(8,128)}) async-done(((f32[128,512]{1,0:T(8,128)}, f32[128,512]{1,0:T(8,128)}, f32[128,512]{1,0:T(8,128)}, f32[128,512]{1,0:T(8,128)}), (f32[128,512]{1,0:T(8,128)}, f32[128,512]{1,0:T(8,128)}, f32[128,512]{1,0:T(8,128)}, ...) | async-done | bytes 1048592 | tf_op jit(solution)/shard_map/psum | solution.py:17
  218.8 11.7 %cholesky.286 = f32[128,128]{1,0:T(8,128)S(1)} custom-call(f32[128,128]{1,0:T(8,128)S(1)} %cholesky.426), custom_call_target="Cholesky" | custom-call | tf_op jit(solution)/shard_map/jit(cholesky)/cholesky | solution.py:56
  230.6 9.8 custom-call.31
  243.0 11.9 %cholesky.305 = f32[128,128]{1,0:T(8,128)S(1)} custom-call(f32[128,128]{1,0:T(8,128)S(1)} %cholesky.430), custom_call_target="Cholesky" | custom-call | tf_op jit(solution)/shard_map/jit(cholesky)/cholesky | solution.py:56
  254.9 9.8 custom-call.32
  266.3 11.7 %cholesky.326 = f32[128,128]{1,0:T(8,128)S(1)} custom-call(f32[128,128]{1,0:T(8,128)S(1)} %cholesky.435), custom_call_target="Cholesky" | custom-call | tf_op jit(solution)/shard_map/jit(cholesky)/cholesky | solution.py:56
  278.0 50.1 %all-reduce.24.cloned.1.call-done = (f32[128,512]{1,0:T(8,128)}, f32[128,512]{1,0:T(8,128)}, f32[128,512]{1,0:T(8,128)}, f32[128,512]{1,0:T(8,128)}, f32[128,512...) async-done(((f32[128,512]{1,0:T(8,128)}, ...) | async-done | bytes 5242896 | tf_op jit(solution)/shard_map/psum | solution.py:23
  328.2 9.8 custom-call.33
  339.4 11.7 %cholesky.343 = f32[128,128]{1,0:T(8,128)S(1)} custom-call(f32[128,128]{1,0:T(8,128)S(1)} %convolution_subtract_fusion.15), custom_call_target="Cholesky" | custom-call | tf_op jit(solution)/shard_map/jit(cholesky)/cholesky | solution.py:56
  357.1 11.7 %while.16 = (s32[]{:T(128)}, f32[512,512]{1,0:T(8,128)}, s32[4,2]{0,1:T(2,128)S(1)}, f32[4,128,128]{2,1,0:T(8,128)S(1)}, s32[]{:T(128)}) while((s32[]{:T(128)}, f32[512,512]{1,0:T(8,128)}, s32[4,2]{0,1:T(2,128)S(1)}, f32[4,128,128]{2,1,0:T(8,128)S(1)}, s32[]{:T(128)}) %tuple.181), condition=%wide.while_cond.8, body=%wide.while_body.8.sunk | while | flops 2 | bytes 131181 | solution.py:35
  358.0 2.2 bitcast_dynamic-update-slice_fusion.11
  360.9 2.2 bitcast_dynamic-update-slice_fusion.11
  363.8 2.2 bitcast_dynamic-update-slice_fusion.11
  368.8 39.3 %custom-call.34 = f32[4,128,128]{1,2,0:T(8,128)S(1)} custom-call(f32[4,128,128]{2,1,0:T(8,128)S(1)} %get-tuple-element.132), custom_call_target="InvertDiagBlocksLowerTriangular" | custom-call | tf_op jit(solution)/shard_map/jit(_solve_triangular)/triangular_solve | solution.py:35
  424.5 2.4 fusion.126
  428.3 3.3 gather_fusion
  431.6 6.1 copy.109
  440.4 20.0 %all-reduce.20.cloned.1.call-done = (f32[1,128,512]{2,1,0:T(8,128)}, f32[1,128,512]{2,1,0:T(8,128)}, f32[1,128,512]{2,1,0:T(8,128)}, f32[1,128,512]{2,1,0:T(8,12...) async-done(((f32[1,128,512]{2,1,0:T(8,128)}, ...) | async-done | bytes 5242896 | tf_op jit(solution)/shard_map/psum | solution.py:23
  480.1 6.3 copy.108
  486.4 2.6 fusion.32
  489.0 2.8 convolution_subtract_fusion.1
  493.1 2.4 convolution_subtract_fusion.3
  496.8 3.5 fusion.21
  501.6 3.0 fusion.127
  504.6 5.9 copy.117
  510.5 2.7 copy.110
  513.2 16.1 %fusion.134 = f32[20,128,5,128]{3,1,2,0:T(8,128)S(1)} fusion(f32[20,128,512,1]{2,1,3,0:T(8,128)} %bitcast.461, f32[5,128,512,1]{2,1,0,3:T(8,128)} %bitcast.477), kind=kOutput, calls=%fused_computation.379 | convolution fusion | flops 10066329600 | bytes 13107200 | tf_op jit(solution)/shard_map/aik,cjk->acij/dot_general | solution.py:62
  529.3 4.2 fusion.3
  538.9 29.1 %all-gather.7.cloned.1.call-done = f32[40,128,128]{2,1,0:T(8,128)} async-done(((f32[5,128,128]{2,1,0:T(8,128)}), f32[40,128,128]{2,1,0:T(8,128)}) %all-gather.7.cloned.1.call-update) | async-done | bytes 2621456 | tf_op jit(solution)/shard_map/all_gather | solution.py:12
  576.1 146.4 %all-reduce.14.cloned.1.call-done = (f32[128,512]{1,0:T(8,128)}, f32[128,512]{1,0:T(8,128)}, f32[128,512]{1,0:T(8,128)}, f32[128,512]{1,0:T(8,128)}) async-done(((f32[128,512]{1,0:T(8,128)}, f32[128,512]{1,0:T(8,128)}, f32[128,512]{1,0:T(8,128)}, f32[128,512]{1,0:T(8,128)}), (f32[128,512]{1,0:T(8,128)}, f32[128,512]{1,0:T(8,128)}, f32[128,512]{1,0:T(8,128)}, ...) | async-done | bytes 1048592 | tf_op jit(solution)/shard_map/psum | solution.py:17
  731.8 11.7 %cholesky.358 = f32[128,128]{1,0:T(8,128)S(1)} custom-call(f32[128,128]{1,0:T(8,128)S(1)} %cholesky.439), custom_call_target="Cholesky" | custom-call | tf_op jit(solution)/shard_map/jit(cholesky)/cholesky | solution.py:56
  743.7 9.8 custom-call.36
  756.0 12.1 %cholesky.377 = f32[128,128]{1,0:T(8,128)S(1)} custom-call(f32[128,128]{1,0:T(8,128)S(1)} %cholesky.443), custom_call_target="Cholesky" | custom-call | tf_op jit(solution)/shard_map/jit(cholesky)/cholesky | solution.py:56
  768.2 9.8 custom-call.37
  779.6 11.7 %cholesky.398 = f32[128,128]{1,0:T(8,128)S(1)} custom-call(f32[128,128]{1,0:T(8,128)S(1)} %cholesky.448), custom_call_target="Cholesky" | custom-call | tf_op jit(solution)/shard_map/jit(cholesky)/cholesky | solution.py:56
  791.3 9.8 custom-call.38
  801.1 38.8 %all-reduce.22.cloned.1.call-done = (f32[128,512]{1,0:T(8,128)}, f32[128,512]{1,0:T(8,128)}, f32[128,512]{1,0:T(8,128)}, f32[128,512]{1,0:T(8,128)}, f32[128,512...) async-done(((f32[128,512]{1,0:T(8,128)}, ...) | async-done | bytes 5242896 | tf_op jit(solution)/shard_map/psum | solution.py:23
  841.4 11.9 %cholesky.415 = f32[128,128]{1,0:T(8,128)S(1)} custom-call(f32[128,128]{1,0:T(8,128)S(1)} %convolution_subtract_fusion.14), custom_call_target="Cholesky" | custom-call | tf_op jit(solution)/shard_map/jit(cholesky)/cholesky | solution.py:56
  860.1 12.1 %while.17 = (s32[]{:T(128)}, f32[512,512]{1,0:T(8,128)}, s32[4,2]{0,1:T(2,128)S(1)}, f32[4,128,128]{2,1,0:T(8,128)S(1)}, s32[]{:T(128)}) while((s32[]{:T(128)}, f32[512,512]{1,0:T(8,128)}, s32[4,2]{0,1:T(2,128)S(1)}, f32[4,128,128]{2,1,0:T(8,128)S(1)}, s32[]{:T(128)}) %tuple.209), condition=%wide.while_cond.8.clone, body=%wide.while_body.8.clone.sunk | while | flops 2 | bytes 131181 | solution.py:35
  860.8 2.4 bitcast_dynamic-update-slice_fusion.12
  863.8 2.4 bitcast_dynamic-update-slice_fusion.12
  866.9 2.4 bitcast_dynamic-update-slice_fusion.12
  869.9 2.3 bitcast_dynamic-update-slice_fusion.12
  872.2 39.3 %custom-call.39 = f32[4,128,128]{1,2,0:T(8,128)S(1)} custom-call(f32[4,128,128]{2,1,0:T(8,128)S(1)} %get-tuple-element.134), custom_call_target="InvertDiagBlocksLowerTriangular" | custom-call | tf_op jit(solution)/shard_map/jit(_solve_triangular)/triangular_solve | solution.py:35
  927.8 2.4 fusion.123
  931.7 3.3 gather_fusion.2
  935.0 6.1 copy.127
  943.7 28.7 %all-reduce.18.cloned.1.call-done = (f32[1,128,512]{2,1,0:T(8,128)}, f32[1,128,512]{2,1,0:T(8,128)}, f32[1,128,512]{2,1,0:T(8,128)}, f32[1,128,512]{2,1,0:T(8,12...) async-done(((f32[1,128,512]{2,1,0:T(8,128)}, ...) | async-done | bytes 5242896 | tf_op jit(solution)/shard_map/psum | solution.py:23
  992.1 6.1 copy.126
  998.3 2.6 fusion.30
  1000.8 2.8 convolution_subtract_fusion
  1004.9 2.4 convolution_subtract_fusion.2
  1008.6 3.5 fusion.18
  1013.4 3.0 fusion.124
  1016.4 5.9 copy.135
  1022.3 2.7 copy.128
  1025.0 16.1 %fusion.135 = f32[20,128,5,128]{3,1,2,0:T(8,128)S(1)} fusion(f32[20,128,512,1]{2,1,3,0:T(8,128)} %bitcast.462, f32[5,128,512,1]{2,1,0,3:T(8,128)} %bitcast.478), kind=kOutput, calls=%fused_computation.380 | convolution fusion | flops 10066329600 | bytes 13107200 | tf_op jit(solution)/shard_map/aik,cjk->acij/dot_general | solution.py:62
  1041.2 4.8 fusion.1
  1047.2 3.2 select_bitcast_fusion
  1050.4 8.1 copy.140
  (350 shorter events, 158.2 us)
Async XLA Ops:
  6.5 49.4 %all-gather.5.cloned.1.call-start = ((), (), s32[]{:S(2)}) async-start(), calls=%async_computation | async-start | bytes 2949120 | tf_op jit(solution)/shard_map/all_gather | solution.py:12
  15.5 4.7 copy-start
  20.8 2.8 copy-start.1
  24.6 186.0 %all-reduce.16.cloned.1.call-start = ((), (), s32[]{:S(2)}) async-start(), calls=%async_computation.3 | async-start | bytes 2097152 | tf_op jit(solution)/shard_map/psum | solution.py:17
  60.3 267.7 %all-reduce.24.cloned.1.call-start = ((), (), s32[]{:S(2)}) async-start(), calls=%async_computation.7 | async-start | bytes 10485760 | tf_op jit(solution)/shard_map/psum | solution.py:23
  84.6 375.7 %all-reduce.20.cloned.1.call-start = ((), (), s32[]{:S(2)}) async-start(), calls=%async_computation.5 | async-start | bytes 10485760 | tf_op jit(solution)/shard_map/psum | solution.py:23
  86.4 322.3 %copy-start.9 = (f32[512,640]{1,0:T(8,128)}, f32[512,640]{1,0:T(8,128)S(1)}, u32[]{:S(2)}) copy-start(f32[512,640]{1,0:T(8,128)S(1)} %maximum_bitcast_fusion.2) | copy-start | bytes 3932164
  217.8 1.0 copy-start.16
  328.1 239.9 %all-gather.7.cloned.1.call-start = ((), (), s32[]{:S(2)}) async-start(), calls=%async_computation.1 | async-start | bytes 2949120 | tf_op jit(solution)/shard_map/all_gather | solution.py:12
  408.1 3.8 copy-start.18
  431.6 7.4 copy-start.10
  431.6 7.4 copy-start.12
  460.4 8.7 copy-start.45
  460.4 9.4 copy-start.43
  460.4 10.2 copy-start.41
  460.4 10.9 %copy-start.39 = (f32[1,128,512]{2,1,0:T(8,128)S(1)}, f32[1,128,512]{2,1,0:T(8,128)}, u32[]{:S(2)}) copy-start(f32[1,128,512]{2,1,0:T(8,128)} %get-tuple-element.188) | copy-start | bytes 786436
  460.4 11.6 %copy-start.37 = (f32[1,128,512]{2,1,0:T(8,128)S(1)}, f32[1,128,512]{2,1,0:T(8,128)}, u32[]{:S(2)}) copy-start(f32[1,128,512]{2,1,0:T(8,128)} %get-tuple-element.189) | copy-start | bytes 786436
  460.4 12.4 %copy-start.35 = (f32[1,128,512]{2,1,0:T(8,128)S(1)}, f32[1,128,512]{2,1,0:T(8,128)}, u32[]{:S(2)}) copy-start(f32[1,128,512]{2,1,0:T(8,128)} %get-tuple-element.190) | copy-start | bytes 786436
  462.2 11.3 %copy-start.33 = (f32[1,128,512]{2,1,0:T(8,128)S(1)}, f32[1,128,512]{2,1,0:T(8,128)}, u32[]{:S(2)}) copy-start(f32[1,128,512]{2,1,0:T(8,128)} %get-tuple-element.191) | copy-start | bytes 786436
  463.9 10.3 copy-start.31
  465.6 9.4 copy-start.29
  467.4 8.3 copy-start.27
  469.1 7.3 copy-start.26
  469.8 7.4 copy-start.25
  470.5 7.4 copy-start.24
  471.3 7.3 copy-start.23
  472.0 7.3 copy-start.22
  480.1 6.3 copy-start.19
  489.0 4.1 copy-start.2
  495.5 6.1 slice-start.2
  496.8 4.8 slice-start.3
  513.2 16.1 %slice-start = ((s8[6553600]{0:T(1024)(128)(4,1)}), s8[4194304]{0:T(1024)(128)(4,1)S(1)}, s32[]{:S(2)}) async-start(s8[6553600]{0:T(1024)(128)(4,1)} %bitcast.455), calls=%async_computation.8 | async-start | bytes 8388608
  513.2 16.1 %slice-start.1 = ((s8[6553600]{0:T(1024)(128)(4,1)}), s8[2359296]{0:T(1024)(128)(4,1)S(1)}, s32[]{:S(2)}) async-start(s8[6553600]{0:T(1024)(128)(4,1)} %bitcast.455), calls=%async_computation.9 | async-start | bytes 4718592
  513.2 16.1 %copy-start.5 = (bf16[2560,512]{1,0:T(8,128)(2,1)S(1)}, bf16[2560,512]{1,0:T(8,128)(2,1)}, u32[]{:S(2)}) copy-start(bf16[2560,512]{1,0:T(8,128)(2,1)} %copy.110) | copy-start | bytes 7864324
  529.3 4.2 copy-start.7
  538.8 183.6 %all-reduce.14.cloned.1.call-start = ((), (), s32[]{:S(2)}) async-start(), calls=%async_computation.2 | async-start | bytes 2097152 | tf_op jit(solution)/shard_map/psum | solution.py:17
  572.1 267.9 %all-reduce.22.cloned.1.call-start = ((), (), s32[]{:S(2)}) async-start(), calls=%async_computation.6 | async-start | bytes 10485760 | tf_op jit(solution)/shard_map/psum | solution.py:23
  573.7 398.7 %all-reduce.18.cloned.1.call-start = ((), (), s32[]{:S(2)}) async-start(), calls=%async_computation.4 | async-start | bytes 10485760 | tf_op jit(solution)/shard_map/psum | solution.py:23
  576.1 335.9 %copy-start.8 = (f32[512,640]{1,0:T(8,128)}, f32[512,640]{1,0:T(8,128)S(1)}, u32[]{:S(2)}) copy-start(f32[512,640]{1,0:T(8,128)S(1)} %maximum_bitcast_fusion.4) | copy-start | bytes 3932164
  730.8 1.0 copy-start.17
  911.5 3.8 copy-start.20
  935.0 7.4 copy-start.11
  935.0 7.4 copy-start.13
  972.4 8.7 copy-start.51
  972.4 9.4 copy-start.50
  972.4 10.2 copy-start.49
  972.4 10.9 %copy-start.48 = (f32[1,128,512]{2,1,0:T(8,128)S(1)}, f32[1,128,512]{2,1,0:T(8,128)}, u32[]{:S(2)}) copy-start(f32[1,128,512]{2,1,0:T(8,128)} %get-tuple-element.168) | copy-start | bytes 786436
  972.4 11.6 %copy-start.47 = (f32[1,128,512]{2,1,0:T(8,128)S(1)}, f32[1,128,512]{2,1,0:T(8,128)}, u32[]{:S(2)}) copy-start(f32[1,128,512]{2,1,0:T(8,128)} %get-tuple-element.169) | copy-start | bytes 786436
  972.4 12.4 %copy-start.46 = (f32[1,128,512]{2,1,0:T(8,128)S(1)}, f32[1,128,512]{2,1,0:T(8,128)}, u32[]{:S(2)}) copy-start(f32[1,128,512]{2,1,0:T(8,128)} %get-tuple-element.170) | copy-start | bytes 786436
  974.2 11.3 %copy-start.44 = (f32[1,128,512]{2,1,0:T(8,128)S(1)}, f32[1,128,512]{2,1,0:T(8,128)}, u32[]{:S(2)}) copy-start(f32[1,128,512]{2,1,0:T(8,128)} %get-tuple-element.171) | copy-start | bytes 786436
  975.9 10.3 copy-start.42
  977.7 9.3 copy-start.40
  979.4 8.4 copy-start.38
  981.1 7.3 copy-start.36
  981.8 7.3 copy-start.34
  982.6 7.3 copy-start.32
  983.3 7.4 copy-start.30
  984.1 7.3 copy-start.28
  992.1 6.1 copy-start.21
  1000.8 4.1 copy-start.3
  1007.3 6.1 slice-start.4
  1008.6 4.8 slice-start.5
  1025.0 16.1 %copy-start.4 = (bf16[2560,512]{1,0:T(8,128)(2,1)S(1)}, bf16[2560,512]{1,0:T(8,128)(2,1)}, u32[]{:S(2)}) copy-start(bf16[2560,512]{1,0:T(8,128)(2,1)} %copy.128) | copy-start | bytes 7864324
  1041.1 4.9 copy-start.6
  (2 other events, 1.5 us)
Sparse Core Ops, SparseCore 0:
  24.7 31.1 all-gather.4
  60.4 150.0 all-reduce.15
  214.4 113.5 all-reduce.23
  331.9 128.4 all-reduce.19
  538.9 28.9 all-gather.6
  572.3 150.1 all-reduce.13
  726.3 113.6 all-reduce.21
  844.0 128.3 all-reduce.17
where the time goes:
time: 1080 us; the launch traced here: 1070 us
  waiting for transfers between devices  440 us (41%)
  other arithmetic  282 us (26%)
  local copies, waits for them, and re-layouts  175 us (16%)
  matrix products  97.3 us (9%)
  between operations  70.4 us (7%)
    psum x2, waiting for transfers between devices, spread(): return lax.psum(kept, axis)  271 us
    another operation x29, other arithmetic, factor_panel(): lower_block = jnp.linalg.cholesky(sym)  158 us
    psum x4, waiting for transfers between devices, from_root(): shard = lax.psum(shard, axis)  138 us
    another operation x5, other arithmetic, solve_rows(): jax.scipy.linalg.solve_triangular(lower_block, flat.T, lower=True)  81.1 us
    unnamed x161, local copies, waits for them, and re-layouts  59.2 us
    another operation x28, matrix products, solve_rows(): jax.scipy.linalg.solve_triangular(lower_block, flat.T, lower=True)  45.1 us
    dot_general x2, matrix products, apply_update(): jnp.einsum('aik,cjk->acij', left, right, precision=lax.Precision.HIGHEST)  32.2 us
    all_gather x2, waiting for transfers between devices, picked(): lax.all_gather(shard, axis)  31.9 us
  transfers between devices with their start and end apart: 8, of which 8 were waited for; matrix products, arithmetic and copies ran while one was open for 34% of the time, Pallas kernels for 0%

commit v1 on v0

v1 whole, which is shorter than its diff:
```python
import jax
import jax.numpy as jnp
from jax import lax
from jax.experimental import pallas as pl
from jax.experimental.pallas import tpu as pltpu
from jax.sharding import Mesh
from jax.sharding import PartitionSpec as P

F32 = jnp.float32
BF16 = jnp.bfloat16
MESH = pl.DeviceIdType.MESH
PT = 4
HI = lax.Precision.HIGHEST
SUB = 32

def halves(v):
    high = v.astype(BF16)
    return high, (v - high.astype(F32)).astype(BF16)

NT = (((1,), (1,)), ((), ()))
TN = (((0,), (0,)), ((), ()))
NN = (((1,), (0,)), ((), ()))

def mm(a, b, dims):
    return lax.dot_general(a, b, dims, preferred_element_type=F32)

def mm3(a, b, dims):
    return mm(a[0], b[0], dims) + (mm(a[0], b[1], dims) + mm(a[1], b[0], dims))

def small_inverse(block, first):
    lanes = block.shape[1]
    cols = []
    for k in range(SUB):
        low = 8 * (k // 8)
        cols.append(jnp.broadcast_to(block[low:, first + k:first + k + 1], (SUB - low, lanes)))
    row = lax.broadcasted_iota(jnp.int32, (SUB, lanes), 0)
    lane = lax.broadcasted_iota(jnp.int32, (SUB, lanes), 1)
    right = (row == lane).astype(F32)
    done = []
    for k in range(SUB):
        low = 8 * (k // 8)
        own = cols[k]
        scale = lax.rsqrt(own[k - low:k - low + 1, :])
        factor = own * scale
        solved = right[k - low:k - low + 1, :] * scale
        done.append(solved)
        if k == SUB - 1:
            break
        nxt = 8 * ((k + 1) // 8)
        for m in range(k + 1, SUB):
            base = 8 * (m // 8)
            cols[m] = cols[m] - factor[base - low:, :] * factor[m - low:m - low + 1, :]
        right = right[nxt - low:, :] - factor[nxt - low:, :] * solved
    return jnp.concatenate(done, axis=0)

def factor_block(a_ref, u_ref, w_ref, t_ref):
    n = a_ref.shape[0]
    u_ref[...] = jnp.zeros_like(u_ref)
    w_ref[...] = jnp.zeros_like(w_ref)

    def body(kb, carry):
        here = pl.ds(pl.multiple_of(kb * 128, 128), 128)
        row = lax.broadcasted_iota(jnp.int32, (128, n), 0)
        lane = lax.broadcasted_iota(jnp.int32, (128, n), 1)
        t_ref[:, :n] = a_ref[here, :]
        t_ref[:, n:] = (lane == row + kb * 128).astype(F32)

        @pl.when(kb > 0)
        def _():
            left = halves(u_ref[:, here])
            t_ref[:, :n] -= mm3(left, halves(u_ref[...]), TN)
            t_ref[:, n:] -= mm3(left, halves(w_ref[...]), TN)

        for s in range(128 // SUB):
            rows = slice(s * SUB, (s + 1) * SUB)
            inv = small_inverse(t_ref[rows, here], s * SUB)[:, :SUB]
            both = lax.dot_general(inv, t_ref[rows, :], NN, precision=HI, preferred_element_type=F32)
            out = pl.ds(pl.multiple_of(kb * 128 + s * SUB, SUB), SUB)
            lane2 = lax.broadcasted_iota(jnp.int32, (SUB, n), 1)
            row2 = lax.broadcasted_iota(jnp.int32, (SUB, n), 0) + (kb * 128 + s * SUB)
            u_ref[out, :] = jnp.where(lane2 >= row2, both[:, :n], 0.0)
            w_ref[out, :] = jnp.where(lane2 <= row2, both[:, n:], 0.0)
            if s < 128 // SUB - 1:
                rest = slice((s + 1) * SUB, 128)
                left = halves(u_ref[out, here])
                t_ref[rest, :] -= mm3(left, halves(both), TN)[rest, :]
        return carry

    lax.fori_loop(0, n // 128, body, 0)

NX, NZ, NY, NA, NTC = 4, 8, 4, 5, 8
PR = 136
ZL, RL, FL = 1, 3, 6

def comm_kernel(pay_ref, left, right, lead, ls, lr, zs, xs, rs, rr, ds, dr):
    x, z, y, c = (lax.axis_index(n) for n in ("x", "z", "y", "c"))
    q = 2 * y + c
    xp, xm = lax.rem(x + 1, NX), lax.rem(x + NX - 1, NX)
    zp, zm = lax.rem(z + 1, NZ), lax.rem(z + NZ - 1, NZ)
    yp, ym, yo = lax.rem(y + 1, NY), lax.rem(y + NY - 1, NY), lax.rem(y + 2, NY)

    def to(src, dst, send, recv, where):
        return pltpu.make_async_remote_copy(src_ref=src, dst_ref=dst, send_sem=send, recv_sem=recv,
                                            device_id=where, device_id_type=MESH)

    barrier = pltpu.get_barrier_semaphore()
    peers = [{"x": xp}, {"x": xm}, {"z": zp}, {"z": zm}, {"y": yp}, {"y": ym}, {"c": 1 - c}]
    for p in peers:
        pl.semaphore_signal(barrier, inc=1, device_id=p, device_id_type=MESH)
    pl.semaphore_wait(barrier, len(peers))

    def group_gather(src, slot, send, recv):
        def go(k, i, ref, where):
            to(ref, slot(k), send(k, i), recv(k), where).start()
        def got(k):
            to(src, slot(k), send(k, 0), recv(k), {"c": 1 - c}).wait_recv()
        go(q, 0, src, {"y": yp})
        go(q, 1, src, {"y": ym})
        go(q, 2, src, {"c": 1 - c})
        km, kp, ko = 2 * ym + c, 2 * yp + c, 2 * yo + c
        got(km)
        @pl.when(c == 0)
        def _():
            go(km, 0, slot(km), {"y": yp})
        go(km, 2, slot(km), {"c": 1 - c})
        got(kp)
        @pl.when(c == 1)
        def _():
            go(kp, 0, slot(kp), {"y": ym})
        go(kp, 2, slot(kp), {"c": 1 - c})
        got(ko)
        go(ko, 2, slot(ko), {"c": 1 - c})
        for k in range(NY):
            got(2 * k + 1 - c)

    def group_sent(src, slot, send):
        def sent(k, i):
            to(src, slot(k), send(k, i), send(k, i), {"c": 1 - c}).wait_send()
        km, kp, ko = 2 * ym + c, 2 * yp + c, 2 * yo + c
        for i in range(3):
            sent(q, i)
        @pl.when(c == 0)
        def _():
            sent(km, 0)
        @pl.when(c == 1)
        def _():
            sent(kp, 0)
        for k in (km, kp, ko):
            sent(k, 2)

    left_args = (pay_ref, lambda k: left.at[k], lambda k, i: ls.at[k, i])
    group_gather(*left_args, lambda k: lr.at[k])
    left[pl.ds(q, 1)] = pay_ref[...][None]

    @pl.when(z == q)
    def _():
        right[pl.ds(x, 1)] = left[...][None]

    zd = (lax.rem(z - q + NZ, NZ), lax.rem(q - z + NZ, NZ))
    znext = ({"z": zp}, {"z": zm})
    xnext = ({"x": xp}, {"x": xm})
    xprev = (xm, xp)
    xfar = lax.rem(x + 2, NX)

    def piece(par, n):
        return 2 * lax.rem(n, 4) + par, n // 4

    def landed(src, t, a):
        r = right.at[src, t, a]
        to(r, r, rs.at[t, a, 0], rr.at[src, t, a], {"x": xp}).wait_recv()

    def push(src, t, a, send, where):
        r = right.at[src, t, a]
        to(r, r, send, rr.at[src, t, a], where).start()

    def step(m, carry):
        for par in range(2):
            n = m - zd[par] * ZL
            @pl.when((n >= 0) & (n < 4 * NA))
            def _():
                t, a = piece(par, n)
                @pl.when(zd[par] > 0)
                def _():
                    landed(x, t, a)
                @pl.when(zd[par] < NZ - 1)
                def _():
                    push(x, t, a, zs.at[t, a], znext[par])
                push(x, t, a, xs.at[t, a, 0], {"x": xp})
                push(x, t, a, xs.at[t, a, 1], {"x": xm})
        for par in range(2):
            n = m - zd[par] * ZL - RL
            @pl.when((n >= 0) & (n < 4 * NA))
            def _():
                t, a = piece(par, n)
                landed(xprev[par], t, a)
                push(xprev[par], t, a, rs.at[t, a, 0], xnext[par])
        for par in range(2):
            n = m - zd[par] * ZL - FL
            @pl.when((n >= 0) & (n < 4 * NA))
            def _():
                t, a = piece(par, n)
                landed(xprev[1 - par], t, a)
                landed(xfar, t, a)
        return carry

    split = 4 + 7 * ZL + FL
    last = 4 * NA + 7 * ZL + FL
    lax.fori_loop(0, split, step, 0)

    row = right.at[0, :, 0]
    lead_args = (row, lambda k: lead.at[k], lambda k, i: ds.at[k, i])
    group_gather(*lead_args, lambda k: dr.at[k])
    lead[pl.ds(q, 1)] = right[0, :, 0][None]
    lax.fori_loop(split, last, step, 0)

    group_sent(pay_ref, left_args[1], left_args[2])
    group_sent(row, lead_args[1], lead_args[2])

    def drain(n, carry):
        for par in range(2):
            t, a = piece(par, n)
            r = right.at[0, t, a]
            def sent(s):
                to(r, r, s, s, {"x": xp}).wait_send()
            @pl.when(zd[par] < NZ - 1)
            def _():
                sent(zs.at[t, a])
            sent(xs.at[t, a, 0])
            sent(xs.at[t, a, 1])
            sent(rs.at[t, a, 0])
        return carry
    lax.fori_loop(0, 4 * NA, drain, 0)

def comm(pay):
    V = pl.BlockSpec(memory_space=pltpu.VMEM)
    D = pltpu.SemaphoreType.DMA
    return pl.pallas_call(
        comm_kernel,
        out_shape=[jax.ShapeDtypeStruct(s, F32) for s in ((NTC, NA, PR, 128), (NX, NTC, NA, PR, 128), (NTC, NTC, PR, 128))],
        in_specs=[V], out_specs=[V] * 3,
        scratch_shapes=[D((8, 3)), D((8,)), D((8, 5)), D((8, 5, 2)), D((8, 5, 1)), D((4, 8, 5)), D((8, 3)), D((8,))],
        compiler_params=pltpu.CompilerParams(collective_id=0, has_side_effects=True, vmem_limit_bytes=60 * 2**20),
    )(pay)

def tile_of(lead, i, t):
    return lead[i, t, 8:, :]

def symmetric(tile):
    row = lax.broadcasted_iota(jnp.int32, tile.shape, 0)
    lane = lax.broadcasted_iota(jnp.int32, tile.shape, 1)
    return jnp.where(row >= lane, tile, tile.T)

def fill_symmetric(a_ref, tile):
    for i in range(PT):
        for t in range(i + 1):
            here = slice(i * 128, (i + 1) * 128), slice(t * 128, (t + 1) * 128)
            value = tile(i, t)
            if i == t:
                a_ref[here] = symmetric(value)
            else:
                a_ref[here] = value
                a_ref[here[1], here[0]] = value.T

def chain_kernel(pos, lead, w0h, w0l, p0h, p0l, w1h, w1l, edge, a, u, w, t):
    z, q = pos[0], pos[1]

    def edge_tile(first):
        @pl.when((z >= first) & (z < first + PT) & (q >= first) & (q <= z))
        def _():
            rows = pl.ds(pl.multiple_of((q - first) * 128, 128), 128)
            lanes = pl.ds(pl.multiple_of((z - first) * 128, 128), 128)
            edge[...] = u[rows, lanes].T

    edge[...] = jnp.zeros_like(edge)
    fill_symmetric(a, lambda i, k: tile_of(lead, i, k))
    factor_block(a, u, w, t)
    edge_tile(0)
    w0h[...], w0l[...] = halves(w[...])
    for i in range(PT):
        rows = slice(i * 128, (i + 1) * 128)
        raw = jnp.concatenate([tile_of(lead, PT + i, k) for k in range(PT)], axis=1)
        p0h[rows], p0l[rows] = halves(mm3(halves(raw), (w0h[...], w0l[...]), NT))

    def updated(i, k):
        hi = slice(i * 128, (i + 1) * 128), slice(k * 128, (k + 1) * 128)
        coarse = mm(p0h[hi[0]], p0h[hi[1]], NT)
        extra = mm(p0h[hi[0]], p0l[hi[1]], NT) + mm(p0l[hi[0]], p0h[hi[1]], NT)
        marked = lead[PT + i, PT + k, 0:1, :] > 0.5
        return tile_of(lead, PT + i, PT + k) - coarse - jnp.where(marked, 0.0, extra)

    fill_symmetric(a, updated)
    factor_block(a, u, w, t)
    edge_tile(PT)
    w1h[...], w1l[...] = halves(w[...])

def chain(pos, lead):
    wide = PT * 128
    V = pl.BlockSpec(memory_space=pltpu.VMEM)
    half = jax.ShapeDtypeStruct((wide, wide), BF16)
    return pl.pallas_call(
        chain_kernel,
        out_shape=[half] * 6 + [jax.ShapeDtypeStruct((128, 128), F32)],
        in_specs=[pl.BlockSpec(memory_space=pltpu.SMEM), V],
        out_specs=[V] * 7,
        scratch_shapes=[pltpu.VMEM((wide, wide), F32)] * 3 + [pltpu.VMEM((128, 2 * wide), F32)],
        compiler_params=pltpu.CompilerParams(vmem_limit_bytes=60 * 2**20),
    )(pos, lead)

def finish_kernel(pos, marks, left, right, w0h, w0l, p0h, p0l, w1h, w1l, edge, work, out, lh, ll, rh, rl):
    r, q = pos[2], pos[1]
    group = pl.program_id(0)
    wide = PT * 128

    def solve(read, count, high, low):
        raw = jnp.concatenate(
            [jnp.concatenate([read(m, k)[8:] for k in range(PT)], axis=1) for m in range(count)], axis=0)
        first = halves(mm3(halves(raw), (w0h[...], w0l[...]), NT))
        high[:, :wide], low[:, :wide] = first
        coarse = mm(first[0], p0h[...], NT)
        extra = mm(first[0], p0l[...], NT) + mm(first[1], p0h[...], NT)
        parts = []
        for m in range(count):
            rows = slice(m * 128, (m + 1) * 128)
            row = []
            for k in range(PT):
                lanes = slice(k * 128, (k + 1) * 128)
                piece = read(m, PT + k)
                row.append(piece[8:] - coarse[rows, lanes] - jnp.where(piece[0:1] > 0.5, 0.0, extra[rows, lanes]))
            parts.append(jnp.concatenate(row, axis=1))
        second = halves(mm3(halves(jnp.concatenate(parts, axis=0)), (w1h[...], w1l[...]), NT))
        high[:, wide:], low[:, wide:] = second

    @pl.when(group == 0)
    def _():
        solve(lambda m, k: left[k, m], NA, lh, ll)

    solve(lambda m, k: right[m, k, 0], NX, rh, rl)

    def one_row(a, carry):
        i = a * 32 + r

        @pl.when(a >= group)
        def _():
            rows = pl.ds(pl.multiple_of(a * 128, 128), 128)
            own_h, own_l = lh[rows, :], ll[rows, :]
            coarse = mm(own_h, rh[...], NT)
            extra = mm(own_h, rl[...], NT) + mm(own_l, rh[...], NT)
            for m in range(NX):
                lanes = slice(m * 128, (m + 1) * 128)
                j = group * 32 + m * 8 + q
                mark = marks[a, group * NX + m]
                tile = work[a, m]
                exact = tile - (coarse[:, lanes] + extra[:, lanes])
                rough = tile.astype(BF16).astype(F32) - coarse[:, lanes]
                rough = rough.astype(BF16).astype(F32)
                value = jnp.where(mark == 1, rough, exact)
                out[a, m] = jnp.where(i >= j, value, 0.0)

        @pl.when(a < group)
        def _():
            out[a] = jnp.zeros((NX, 128, 128), F32)
        return carry

    lax.fori_loop(0, NA, one_row, 0)

    @pl.when(group == 0)
    def _():
        lanes = pl.ds(pl.multiple_of(q * 128, 128), 128)
        for a in range(NA):
            i = a * 32 + r
            rows = slice(a * 128, (a + 1) * 128)
            value = lh[rows, lanes].astype(F32) + ll[rows, lanes].astype(F32)
            if a == 0:
                value = jnp.where((i < 2 * PT) & (i // PT == q // PT), edge[...], value)
            value = jnp.where(marks[a, 0] == 1, value.astype(BF16).astype(F32), value)
            out[a, 0] = jnp.where(i >= q, value, 0.0)

def finish(pos, marks, left, right, parts, work):
    wide = PT * 128
    S = pl.BlockSpec(memory_space=pltpu.SMEM)
    whole = lambda s: pl.BlockSpec(s, lambda g: (0,) * len(s))
    tiles = pl.BlockSpec((NA, NX, 128, 128), lambda g: (0, g, 0, 0))
    return pl.pallas_call(
        finish_kernel,
        grid=(NA,),
        out_shape=jax.ShapeDtypeStruct(work.shape, F32),
        in_specs=[S, S, whole(left.shape), pl.BlockSpec((NX, NTC, 1, PR, 128), lambda g: (0, 0, g, 0, 0))]
        + [whole(v.shape) for v in parts] + [tiles],
        out_specs=tiles,
        scratch_shapes=[pltpu.VMEM((NA * 128, 2 * wide), BF16)] * 2 + [pltpu.VMEM((NX * 128, 2 * wide), BF16)] * 2,
        compiler_params=pltpu.CompilerParams(vmem_limit_bytes=60 * 2**20, dimension_semantics=("arbitrary",)),
    )(pos, marks, left, right, *parts, work)

def on_device(matrix, flags):
    x, z, y, c = (lax.axis_index(n) for n in ("x", "z", "y", "c"))
    tiles = matrix.reshape(NA, NA * NX, 128, 128)
    marks = flags.reshape(NA, NA * NX)
    first = marks[:, 0][:, None, None]
    own = tiles[:, 0]
    own = jnp.where(first == 1, lax.reduce_precision(own, 8, 7), own)
    pay = jnp.concatenate([jnp.broadcast_to(first.astype(F32), (NA, 8, 128)), own], axis=1)
    left, right, lead = comm(pay)
    pos = jnp.stack([jnp.where(x == 0, z, 4 * PT), 2 * y + c, 8 * x + z]).astype(jnp.int32)
    parts = chain(pos, lead)
    return finish(pos, marks, left, right, parts, tiles).reshape(matrix.shape)

def solution(mesh):
    finer = Mesh(mesh.devices.reshape(NX, NZ, NY, 2), ("x", "z", "y", "c"))
    rows, cols = ("x", "z"), ("y", "c")
    return jax.shard_map(
        on_device, mesh=finer, in_specs=(P(None, rows, None, cols, None, None), P(None, rows, None, cols)),
        out_specs=P(None, rows, None, cols, None, None), check_vma=False)
```

time: 1080 us -> 244 us (0.23); the launches traced: 1070 us -> 241 us
  waiting for transfers between devices: 440 us -> 0 us
  other arithmetic: 282 us -> 2.67 us
  Pallas kernels: 0 us -> 238 us
  local copies, waits for them, and re-layouts: 175 us -> 0.76 us
  matrix products: 97.3 us -> 0 us
  between operations: 70.4 us -> 0.02 us
    psum x6 -> x0, waiting for transfers between devices: 408 us -> none  [the longest x2 271 us: spread(): return lax.psum(kept, axis)]
    another operation x34 -> x1, other arithmetic: 240 us -> 0.61 us  [on_device(): jnp.stack([jnp.where(x == 0, z, 4 * PT), 2 * y + c, 8 * x + z])]
    pallas_call x0 -> x3, Pallas kernels: none -> 238 us  [the longest x1 152 us: comm(): pl.pallas_call(comm_kernel, out_shape=[jax.ShapeDtypeStruct(s, F32) for s...]
    unnamed x161 -> x3, local copies, waits for them, and re-layouts: 59.2 us -> 0.69 us
    another operation x40 -> x0, matrix products: 56 us -> none  [the longest x28 45.1 us: solve_rows(): jax.scipy.linalg.solve_triangular(lower_block, flat.T, lower=True)]
    dot_general x4 -> x0, matrix products: 41.3 us -> none  [the longest x2 32.2 us: apply_update(): jnp.einsum('aik,cjk->acij', left, right, precision=lax.Precision.HIGHEST)]
    all_gather x2 -> x0, waiting for transfers between devices: 31.9 us -> none  [picked(): lax.all_gather(shard, axis)]
    gather x10 -> x0, local copies, waits for them, and re-layouts: 25.9 us -> none  [with_block(): lower_block.reshape(PT, solved.shape[1], solved.shape[2])[offset]]
  transfers between devices with their start and end apart: 8 -> 0, of which waited for: 8 -> 0; matrix products, arithmetic and copies ran while one was open for 34% -> 0% of each run, Pallas kernels for 0% -> 0%
where the time goes in v1:
time: 244 us; the launch traced here: 241 us
  Pallas kernels  238 us (98%)
  other arithmetic  2.67 us (1%)
    pallas_call x1, Pallas kernels, comm(): pl.pallas_call(comm_kernel, out_shape=[jax.ShapeDtypeStruct(s, F32) for s...  152 us
    pallas_call x1, Pallas kernels, chain(): pl.pallas_call(chain_kernel, out_shape=[half] * 6 + [jax.ShapeDtypeStruct...  45.7 us
    pallas_call x1, Pallas kernels, finish(): pl.pallas_call(finish_kernel, grid=(NA,), out_shape=jax.ShapeDtypeStruct(...  40 us

profile of v1, /device:TPU:32, one launch (start us, length us, event | category | flops | bytes accessed | tf_op | source)
XLA Modules:
  0.0 241.1 jit_solution(14466404971753080278)
XLA Ops:
  0.0 0.6 pad_add_fusion.pos
  0.6 0.7 copy.7
  1.3 0.0 copy-start
  1.3 0.1 compare_reduce_fusion
  1.4 0.1 convert_reduce_fusion
  1.5 0.1 broadcast_in_dim.13
  1.6 1.1 reduce-precision_select_fusion
  2.7 0.8 pad_maximum_fusion.pay_ref
  3.4 151.9 %shard_map.28 = (f32[8,5,136,128]{3,2,1,0:T(8,128)}, f32[4,8,5,136,128]{4,3,2,1,0:T(8,128)}, f32[8,8,136,128]{3,2,1,0:T(8,128)}) custom-call(f32[5,136,128]{2,1,0:T(8,128)} %pad_maximum_fusion.pay_ref), custom_call_target="tpu_custom_call" | custom-call | tf_op jit(solution)/shard_map/pallas_call | solution.py:237
  155.4 45.7 %shard_map.29 = (bf16[512,512]{1,0:T(8,128)(2,1)}, bf16[512,512]{1,0:T(8,128)(2,1)}, bf16[512,512]{1,0:T(8,128)(2,1)}, bf16[512,512]{1,0:T(8,128)(2,1)}, bf16[51...) custom-call(s32[3]{0:T(128)} %pad_add_fusion.pos, f32[8,8,136,128]{3,2,1,0:T(8,128)} %get-tuple-element.17.lead), custom_call_target="tpu_custom_call" | custom-call | tf_op jit(solution)/shard_map/pallas_call | solution.py:300
  201.1 0.0 copy-done
  201.1 40.0 %shard_map.30 = f32[5,20,128,128]{3,2,1,0:T(8,128)} custom-call(s32[3]{0:T(128)} %pad_add_fusion.pos, s32[5,20]{1,0:T(8,128)} %bitcast.18, f32[8,5,136,128]{3,2,1,0:T(8,128)} %get-tuple-element.15.left, f32[4,8,5,136,128]{4,3,2,1,0:T(8,128)} %get-tuple-element.16.right, bf16[512,512]{1,0:T(8,128)(2,1)} %get-tuple-element.18.w0h, ...), custom_call_target="tpu_custom_call" | custom-call | tf_op jit(solution)/shard_map/pallas_call | solution.py:383
Async XLA Ops:
  1.3 199.8 %copy-start = (s32[5,1,20,1]{2,0,1,3:T(8,128)}, s32[5,1,20,1]{2,0,1,3:T(8,128)S(1)}, u32[]{:S(2)}) copy-start(s32[5,1,20,1]{2,0,1,3:T(8,128)S(1)} %copy.7) | copy-start | bytes 1204

commit v2 on v1

v2 whole, which is shorter than its diff:
```python
import jax
import jax.numpy as jnp
from jax import lax
from jax.experimental import pallas as pl
from jax.experimental.pallas import tpu as pltpu
from jax.sharding import Mesh
from jax.sharding import PartitionSpec as P

F32 = jnp.float32
BF16 = jnp.bfloat16
MESH = pl.DeviceIdType.MESH
PT = 4
HI = lax.Precision.HIGHEST
SUB = 32

def halves(v):
    high = v.astype(BF16)
    return high, (v - high.astype(F32)).astype(BF16)

NT = (((1,), (1,)), ((), ()))
TN = (((0,), (0,)), ((), ()))
NN = (((1,), (0,)), ((), ()))

def mm(a, b, dims):
    return lax.dot_general(a, b, dims, preferred_element_type=F32)

def mm6(a, b, dims):
    return lax.dot_general(a, b, dims, precision=HI, preferred_element_type=F32)

def mm3(a, b, dims):
    return mm(a[0], b[0], dims) + (mm(a[0], b[1], dims) + mm(a[1], b[0], dims))

def small_inverse(block):
    lanes = block.shape[1]
    groups = []
    for g in range(SUB // 8):
        low = 8 * g
        groups.append([jnp.broadcast_to(block[low:, low + e:low + e + 1], (SUB - low, lanes)) for e in range(8)])
    row = lax.broadcasted_iota(jnp.int32, (SUB, lanes), 0)
    lane = lax.broadcasted_iota(jnp.int32, (SUB, lanes), 1)
    right = (row == lane).astype(F32)
    done = []
    cols = [jnp.stack(g, axis=0) for g in groups]
    for g in range(SUB // 8):
        for e in range(8):
            own = cols[g][0]
            scale = lax.rsqrt(own[e:e + 1])
            factor = own * scale
            solved = right[e:e + 1] * scale
            done.append(solved)
            right = right - factor * solved
            if e < 7:
                cols[g] = cols[g][1:] - factor[None] * factor[e + 1:8][:, None]
            for h in range(g + 1, SUB // 8):
                off = 8 * (h - g)
                cols[h] = cols[h] - factor[off:][None] * factor[off:off + 8][:, None]
        right = right[8:]
    return jnp.concatenate(done, axis=0)

def factor_unit(kb, s, a_ref, u_ref, w_ref, t_ref):
    n = a_ref.shape[0]
    here = pl.ds(pl.multiple_of(kb * 128, 128), 128)

    @pl.when(s == 0)
    def _():
        row = lax.broadcasted_iota(jnp.int32, (128, n), 0)
        lane = lax.broadcasted_iota(jnp.int32, (128, n), 1)
        t_ref[:, :n] = a_ref[here, :]
        t_ref[:, n:] = (lane == row + kb * 128).astype(F32)

        @pl.when(kb > 0)
        def _():
            left = u_ref[:, here]
            t_ref[:, :n] -= mm6(left, u_ref[...], TN)
            t_ref[:, n:] -= mm6(left, w_ref[...], TN)

    rows = pl.ds(pl.multiple_of(s * SUB, SUB), SUB)
    out = pl.ds(pl.multiple_of(kb * 128 + s * SUB, SUB), SUB)
    inv = small_inverse(pltpu.roll(t_ref[rows, here], (128 - s * SUB) % 128, 1))[:, :SUB]
    both = mm6(inv, t_ref[rows, :], NN)
    lane = lax.broadcasted_iota(jnp.int32, (SUB, n), 1)
    row = lax.broadcasted_iota(jnp.int32, (SUB, n), 0) + (kb * 128 + s * SUB)
    u_ref[out, :] = jnp.where(lane >= row, both[:, :n], 0.0)
    w_ref[out, :] = jnp.where(lane <= row, both[:, n:], 0.0)
    left = u_ref[out, here]
    t_ref[...] -= mm6(left, both, TN)

def tile_of(lead, i, t):
    return lead[t, i, 8:, :]

def symmetric(tile):
    row = lax.broadcasted_iota(jnp.int32, tile.shape, 0)
    lane = lax.broadcasted_iota(jnp.int32, tile.shape, 1)
    return jnp.where(row >= lane, tile, tile.T)

def fill_symmetric(a_ref, tile):
    for i in range(PT):
        for t in range(i + 1):
            here = slice(i * 128, (i + 1) * 128), slice(t * 128, (t + 1) * 128)
            value = tile(i, t)
            if i == t:
                a_ref[here] = symmetric(value)
            else:
                a_ref[here] = value
                a_ref[here[1], here[0]] = value.T

def edge_tile(z, q, first, edge, u):
    @pl.when((z >= first) & (z < first + PT) & (q >= first) & (q <= z))
    def _():
        rows = pl.ds(pl.multiple_of(lax.rem(q, PT) * 128, 128), 128)
        lanes = pl.ds(pl.multiple_of(lax.rem(z, PT) * 128, 128), 128)
        edge[...] = u[rows, lanes].T

def chain_open(lead, edge, a, u, w):
    edge[...] = jnp.zeros_like(edge)
    fill_symmetric(a, lambda i, k: tile_of(lead, i, k))
    u[...] = jnp.zeros_like(u)
    w[...] = jnp.zeros_like(w)

def chain_turn(z, q, lead, w0h, w0l, p0h, p0l, edge, a, u, w):
    edge_tile(z, q, 0, edge, u)
    w0h[...], w0l[...] = halves(w[...])
    for i in range(PT):
        rows = slice(i * 128, (i + 1) * 128)
        raw = jnp.concatenate([tile_of(lead, PT + i, k) for k in range(PT)], axis=1)
        p0h[rows], p0l[rows] = halves(mm3(halves(raw), (w0h[...], w0l[...]), NT))

    def updated(i, k):
        hi = slice(i * 128, (i + 1) * 128), slice(k * 128, (k + 1) * 128)
        coarse = mm(p0h[hi[0]], p0h[hi[1]], NT)
        extra = mm(p0h[hi[0]], p0l[hi[1]], NT) + mm(p0l[hi[0]], p0h[hi[1]], NT)
        marked = lead[PT + k, PT + i, 0:1, :] > 0.5
        return tile_of(lead, PT + i, PT + k) - coarse - jnp.where(marked, 0.0, extra)

    fill_symmetric(a, updated)
    u[...] = jnp.zeros_like(u)
    w[...] = jnp.zeros_like(w)

def chain_close(z, q, w1h, w1l, edge, u, w):
    edge_tile(z, q, PT, edge, u)
    w1h[...], w1l[...] = halves(w[...])

UNITS = 2 * PT * 128 // SUB

def chain_unit(n, z, q, lead, outs, edge, a, u, w, t):
    half = UNITS // 2

    @pl.when(n == half)
    def _():
        chain_turn(z, q, lead, *outs[:4], edge, a, u, w)
    k = lax.rem(n, half)
    factor_unit(k // (128 // SUB), lax.rem(k, 128 // SUB), a, u, w, t)

NX, NZ, NY, NA, NTC = 4, 8, 4, 5, 8
PR = 136
ZL, RL, FL, OFF = 1, 2, 4, 1
NS = 3
OPEN = 3
PER = 2

def move_kernel(with_chain, pay_ref, left, right, lead, w0h, w0l, p0h, p0l, w1h, w1l, edge,
                a_ref, u_ref, w_ref, t_ref, ls, lr, zs, xs, rs, rr, qs, qr, gs, gr, hs, hr):
    x, z, y, c = (lax.axis_index(n) for n in ("x", "z", "y", "c"))
    q = 2 * y + c
    xp, xm, xfar = lax.rem(x + 1, NX), lax.rem(x + NX - 1, NX), lax.rem(x + 2, NX)
    zp, zm = lax.rem(z + 1, NZ), lax.rem(z + NZ - 1, NZ)
    yp, ym, yo = lax.rem(y + 1, NY), lax.rem(y + NY - 1, NY), lax.rem(y + 2, NY)
    other = {"c": 1 - c}

    def to(src, dst, send, recv, where):
        return pltpu.make_async_remote_copy(src_ref=src, dst_ref=dst, send_sem=send, recv_sem=recv,
                                            device_id=where, device_id_type=MESH)

    barrier = pltpu.get_barrier_semaphore()
    peers = [{"x": xp}, {"x": xm}, {"z": zp}, {"z": zm}, {"y": yp}, {"y": ym}, other]
    for p in peers:
        pl.semaphore_signal(barrier, inc=1, device_id=p, device_id_type=MESH)
    pl.semaphore_wait(barrier, len(peers))

    class Gather:
        def __init__(self, own, slot, send, recv, limit):
            self.own, self.slot, self.send, self.recv, self.limit = own, slot, send, recv, limit

        def on(self, k, fn):
            if self.limit == NTC:
                fn()
            else:
                pl.when(k < self.limit)(fn)

        def copy(self, src, k, i, where):
            return to(src, self.slot(k), self.send.at[k, i], self.recv.at[k], where)

        def got(self, k):
            self.copy(self.slot(k), k, 0, other).wait_recv()

        def open(self):
            def go():
                for i, where in enumerate(({"y": yp}, {"y": ym}, other)):
                    self.copy(self.own, q, i, where).start()
            self.on(q, go)

        def pass_on(self):
            for k, core, where in ((2 * ym + c, 0, {"y": yp}), (2 * yp + c, 1, {"y": ym})):
                def go(k=k, core=core, where=where):
                    self.got(k)
                    @pl.when(c == core)
                    def _():
                        self.copy(self.slot(k), k, 0, where).start()
                    self.copy(self.slot(k), k, 2, other).start()
                self.on(k, go)

        def share(self):
            k = 2 * yo + c
            def go():
                self.got(k)
                self.copy(self.slot(k), k, 2, other).start()
            self.on(k, go)

        def close(self):
            for n in range(NY):
                k = 2 * n + 1 - c
                self.on(k, lambda k=k: self.got(k))

        def drain(self):
            def sent(k, i):
                self.copy(self.slot(k), k, i, other).wait_send()
            self.on(q, lambda: [sent(q, i) for i in range(3)] and None)
            for k, core in ((2 * ym + c, 0), (2 * yp + c, 1)):
                def go(k=k, core=core):
                    pl.when(c == core)(lambda: sent(k, 0))
                    sent(k, 2)
                self.on(k, go)
            self.on(2 * yo + c, lambda: sent(2 * yo + c, 2))

    sides = Gather(pay_ref, lambda k: left.at[k], ls, lr, NTC)
    upper = Gather(lead.at[q, pl.ds(0, PT)], lambda k: lead.at[k, pl.ds(0, PT)], gs, gr, PT)
    lower = Gather(lead.at[q, pl.ds(PT, PT)], lambda k: lead.at[k, pl.ds(PT, PT)], hs, hr, NTC)

    sides.open()

    mine = pay_ref.at[0]
    def tip(row, send, where, src=None):
        slot = lead.at[q, row]
        return to(slot if src is None else src, slot, qs.at[send], qr.at[row], where)

    @pl.when(x == 0)
    def _():
        tip(z, 0, {"x": xp}, mine).start()
        tip(z, 1, {"x": xm}, mine).start()
        lead[pl.ds(q, 1), pl.ds(z, 1)] = pay_ref[0][None, None]
        tip(z, 2, {"z": zp}, mine).start()
        tip(z, 6, {"z": zm}, mine).start()

    @pl.when(x > 0)
    def _():
        tip(z, 0, other).wait_recv()
        @pl.when(x == 1)
        def _():
            tip(z, 0, {"x": xp}).start()
        tip(z, 2, {"z": zp}).start()
        tip(z, 6, {"z": zm}).start()

    for h in range(1, 5):
        row = lax.rem(z - h + NZ, NZ)
        tip(row, 0, other).wait_recv()
        if h < 4:
            tip(row, 2 + h, {"z": zp}).start()
            row = lax.rem(z + h, NZ)
            tip(row, 0, other).wait_recv()
            if h < 3:
                tip(row, 6 + h, {"z": zm}).start()

    upper.open()
    sides.pass_on()
    lower.open()
    sides.share()
    sides.close()
    left[pl.ds(q, 1)] = pay_ref[...][None]

    zd = (lax.rem(z - q + NZ, NZ), lax.rem(q - z + NZ, NZ))
    znext = ({"z": zp}, {"z": zm})
    xnext = ({"x": xp}, {"x": xm})
    xprev = (xm, xp)

    def landed(src, t, a):
        r = right.at[src, t, a]
        to(r, r, rs.at[t, a], rr.at[src, t, a], other).wait_recv()

    def push(src, t, a, send, where, ref=None):
        r = right.at[src, t, a]
        to(r if ref is None else ref, r, send, rr.at[src, t, a], where).start()

    def inside(n, low, high, fn):
        pl.when((n >= low) & (n < high))(fn)

    def near(par, n):
        t, a = 2 * lax.rem(n, 4) + par, n // 4

        def send(ref):
            @pl.when(zd[par] < NZ - 1)
            def _():
                push(x, t, a, zs.at[x, t, a], znext[par], ref)
            push(x, t, a, xs.at[t, a, 0], {"x": xp}, ref)
            push(x, t, a, xs.at[t, a, 1], {"x": xm}, ref)

        @pl.when(zd[par] == 0)
        def _():
            send(left.at[t, a])

        @pl.when(zd[par] > 0)
        def _():
            landed(x, t, a)
            send(None)

    def relay(par, n):
        t, a = 2 * lax.rem(n, 4) + par, n // 4
        landed(xprev[par], t, a)
        push(xprev[par], t, a, rs.at[t, a], xnext[par])

    def last_landed(par, n):
        t, a = 2 * lax.rem(n, 4) + par, n // 4
        landed(xprev[1 - par], t, a)
        landed(xfar, t, a)

    def spread(par, n):
        t, a = 2 * lax.rem(n, 4) + par, n // 4
        push(x, t, a, xs.at[t, a, 0], {"x": xp}, left.at[t, a])
        push(x, t, a, xs.at[t, a, 1], {"x": xm}, left.at[t, a])

    far = 4 * (NA - NS)

    def stream(par, k):
        rel, j = k // far, lax.rem(k, far)
        t, a = 2 * lax.rem(j, 4) + par, NS + j // 4
        sign = 3 if par == 0 else 1
        src = lax.rem(x + jnp.where(rel == 0, 0, jnp.where(rel == 1, sign, jnp.where(rel == 2, 4 - sign, 2))), NX)

        @pl.when((zd[par] > 0) | (rel > 1))
        def _():
            landed(src, t, a)

        @pl.when(zd[par] < NZ - 1)
        def _():
            own = (zd[par] == 0) & (rel == 0)
            @pl.when(own)
            def _():
                push(src, t, a, zs.at[src, t, a], znext[par], left.at[t, a])

            @pl.when(jnp.logical_not(own))
            def _():
                push(src, t, a, zs.at[src, t, a], znext[par])

    def step(m, carry):
        for par in range(2):
            n = m - zd[par] * ZL
            inside(n, 0, 4 * NS, lambda: near(par, n))
            @pl.when((zd[par] == 0) & (n < far // 2))
            def _():
                spread(par, 4 * NS + 2 * n)
                spread(par, 4 * NS + 2 * n + 1)
            inside(n - RL, 0, 4 * NS, lambda: relay(par, n - RL))
            @pl.when((zd[par] == 0) & (n >= RL) & (n < far // 2 + RL))
            def _():
                relay(par, 4 * NS + 2 * (n - RL))
                relay(par, 4 * NS + 2 * (n - RL) + 1)
            for i in range(3):
                k = 3 * (n - OFF) + i
                inside(k, 0, NX * far, lambda: stream(par, k))
            inside(n - FL, 0, 4 * NS, lambda: last_landed(par, n - FL))
        pl.when(m == 1)(upper.pass_on)
        @pl.when(m == OPEN)
        def _():
            upper.share()
            upper.close()
            chain_open(lead, edge, a_ref, u_ref, w_ref)
        pl.when(m == OPEN + 1)(lower.pass_on)
        pl.when(m == OPEN + 3)(lower.share)
        pl.when(m == OPEN + 5)(lower.close)
        for i in range(PER):
            unit = PER * (m - OPEN) + i
            inside(unit, 0, UNITS, lambda: chain_unit(
                unit, jnp.where(x == 0, z, 4 * PT), q, lead, (w0h, w0l, p0h, p0l), edge, a_ref, u_ref, w_ref, t_ref))
        return carry

    steps = max(4 * NS + 7 * ZL + FL, OPEN + UNITS // PER)
    lax.fori_loop(0, steps, step, 0)
    chain_close(jnp.where(x == 0, z, 4 * PT), q, w1h, w1l, edge, u_ref, w_ref)

    @pl.when(z == q)
    def _():
        right[pl.ds(x, 1)] = left[...][None]

    sides.drain()
    upper.drain()
    lower.drain()

    def tip_sent(i):
        tip(z, i, other).wait_send()

    pl.when(x <= 1)(lambda: tip_sent(0))
    pl.when(x == 0)(lambda: tip_sent(1))
    for i in range(2, 9):
        tip_sent(i)

    def drain(n, carry):
        for par in range(2):
            t, a = 2 * lax.rem(n, 4) + par, n // 4
            def sent(s):
                r = right.at[0, t, a]
                to(r, r, s, s, other).wait_send()

            @pl.when((n < 4 * NS) | (zd[par] == 0))
            def _():
                sent(xs.at[t, a, 0])
                sent(xs.at[t, a, 1])
                sent(rs.at[t, a])

            @pl.when(zd[par] < NZ - 1)
            def _():
                @pl.when(n < 4 * NS)
                def _():
                    sent(zs.at[x, t, a])

                @pl.when(n >= 4 * NS)
                def _():
                    for k in range(NX):
                        sent(zs.at[k, t, a])
        return carry
    lax.fori_loop(0, 4 * NA, drain, 0)

def move(pay):
    V = pl.BlockSpec(memory_space=pltpu.VMEM)
    D = pltpu.SemaphoreType.DMA
    wide = PT * 128
    half = jax.ShapeDtypeStruct((wide, wide), BF16)
    shape = lambda *s: jax.ShapeDtypeStruct(s, F32)
    return pl.pallas_call(
        lambda *r: move_kernel(True, *r[:3], r[10], *r[3:10], *r[11:]),
        out_shape=[shape(NTC, NA, PR, 128), shape(NX, NTC, NA, PR, 128)] + [half] * 6 + [shape(128, 128)],
        in_specs=[V], out_specs=[V] * 9,
        scratch_shapes=[pltpu.VMEM((NTC, NTC, PR, 128), F32)] + [pltpu.VMEM((wide, wide), F32)] * 3
        + [pltpu.VMEM((128, 2 * wide), F32)]
        + [D((8, 3)), D((8,)), D((4, 8, 5)), D((8, 5, 2)), D((8, 5)), D((4, 8, 5)), D((9,)), D((8,)),
           D((8, 3)), D((8,)), D((8, 3)), D((8,))],
        compiler_params=pltpu.CompilerParams(collective_id=0, has_side_effects=True, vmem_limit_bytes=60 * 2**20),
    )(pay)

def finish_kernel(pos, marks, left, right, w0h, w0l, p0h, p0l, w1h, w1l, edge, work, out, lh, ll, rh, rl):
    r, q = pos[2], pos[1]
    group = pl.program_id(0)
    wide = PT * 128

    def solve(read, count, high, low):
        raw = jnp.concatenate(
            [jnp.concatenate([read(m, k)[8:] for k in range(PT)], axis=1) for m in range(count)], axis=0)
        first = halves(mm3(halves(raw), (w0h[...], w0l[...]), NT))
        high[:, :wide], low[:, :wide] = first
        coarse = mm(first[0], p0h[...], NT)
        extra = mm(first[0], p0l[...], NT) + mm(first[1], p0h[...], NT)
        parts = []
        for m in range(count):
            rows = slice(m * 128, (m + 1) * 128)
            row = []
            for k in range(PT):
                lanes = slice(k * 128, (k + 1) * 128)
                piece = read(m, PT + k)
                row.append(piece[8:] - coarse[rows, lanes] - jnp.where(piece[0:1] > 0.5, 0.0, extra[rows, lanes]))
            parts.append(jnp.concatenate(row, axis=1))
        second = halves(mm3(halves(jnp.concatenate(parts, axis=0)), (w1h[...], w1l[...]), NT))
        high[:, wide:], low[:, wide:] = second

    @pl.when(group == 0)
    def _():
        solve(lambda m, k: left[k, m], NA, lh, ll)

    solve(lambda m, k: right[m, k, 0], NX, rh, rl)

    def one_row(a, carry):
        i = a * 32 + r

        @pl.when(a >= group)
        def _():
            rows = pl.ds(pl.multiple_of(a * 128, 128), 128)
            own_h, own_l = lh[rows, :], ll[rows, :]
            coarse = mm(own_h, rh[...], NT)
            extra = mm(own_h, rl[...], NT) + mm(own_l, rh[...], NT)
            for m in range(NX):
                lanes = slice(m * 128, (m + 1) * 128)
                j = group * 32 + m * 8 + q
                mark = marks[a, group * NX + m]
                tile = work[a, m]
                exact = tile - (coarse[:, lanes] + extra[:, lanes])
                rough = tile.astype(BF16).astype(F32) - coarse[:, lanes]
                rough = rough.astype(BF16).astype(F32)
                value = jnp.where(mark == 1, rough, exact)
                out[a, m] = jnp.where(i >= j, value, 0.0)

        @pl.when(a < group)
        def _():
            out[a] = jnp.zeros((NX, 128, 128), F32)
        return carry

    lax.fori_loop(0, NA, one_row, 0)

    @pl.when(group == 0)
    def _():
        lanes = pl.ds(pl.multiple_of(q * 128, 128), 128)
        for a in range(NA):
            i = a * 32 + r
            rows = slice(a * 128, (a + 1) * 128)
            value = lh[rows, lanes].astype(F32) + ll[rows, lanes].astype(F32)
            if a == 0:
                value = jnp.where((i < 2 * PT) & (i // PT == q // PT), edge[...], value)
            value = jnp.where(marks[a, 0] == 1, value.astype(BF16).astype(F32), value)
            out[a, 0] = jnp.where(i >= q, value, 0.0)

def finish(pos, marks, left, right, parts, work):
    wide = PT * 128
    S = pl.BlockSpec(memory_space=pltpu.SMEM)
    whole = lambda s: pl.BlockSpec(s, lambda g: (0,) * len(s))
    tiles = pl.BlockSpec((NA, NX, 128, 128), lambda g: (0, g, 0, 0))
    return pl.pallas_call(
        finish_kernel,
        grid=(NA,),
        out_shape=jax.ShapeDtypeStruct(work.shape, F32),
        in_specs=[S, S, whole(left.shape), pl.BlockSpec((NX, NTC, 1, PR, 128), lambda g: (0, 0, g, 0, 0))]
        + [whole(v.shape) for v in parts] + [tiles],
        out_specs=tiles,
        scratch_shapes=[pltpu.VMEM((NA * 128, 2 * wide), BF16)] * 2 + [pltpu.VMEM((NX * 128, 2 * wide), BF16)] * 2,
        compiler_params=pltpu.CompilerParams(vmem_limit_bytes=60 * 2**20, dimension_semantics=("arbitrary",)),
    )(pos, marks, left, right, *parts, work)

def on_device(matrix, flags):
    x, z, y, c = (lax.axis_index(n) for n in ("x", "z", "y", "c"))
    tiles = matrix.reshape(NA, NA * NX, 128, 128)
    marks = flags.reshape(NA, NA * NX)
    first = marks[:, 0][:, None, None]
    own = tiles[:, 0]
    own = jnp.where(first == 1, lax.reduce_precision(own, 8, 7), own)
    pay = jnp.concatenate([jnp.broadcast_to(first.astype(F32), (NA, 8, 128)), own], axis=1)
    left, right, *parts = move(pay)
    pos = jnp.stack([jnp.where(x == 0, z, 4 * PT), 2 * y + c, 8 * x + z]).astype(jnp.int32)
    return finish(pos, marks, left, right, parts, tiles).reshape(matrix.shape)

def solution(mesh):
    finer = Mesh(mesh.devices.reshape(NX, NZ, NY, 2), ("x", "z", "y", "c"))
    rows, cols = ("x", "z"), ("y", "c")
    return jax.shard_map(
        on_device, mesh=finer, in_specs=(P(None, rows, None, cols, None, None), P(None, rows, None, cols)),
        out_specs=P(None, rows, None, cols, None, None), check_vma=False)
```

time: 244 us -> 210 us (0.86)
  Pallas kernels: 238 us -> 204 us
    pallas_call x2 -> x1, Pallas kernels: 198 us -> 164 us  [move(): pl.pallas_call(lambda *r: move_kernel(True, *r[:3], r[10], *r[3:10], *r[1...]
where the time goes in v2:
time: 210 us; the launch traced here: 208 us
  Pallas kernels  204 us (97%)
  other arithmetic  2.66 us (1%)
    pallas_call x1, Pallas kernels, move(): pl.pallas_call(lambda *r: move_kernel(True, *r[:3], r[10], *r[3:10], *r[1...  164 us
    pallas_call x1, Pallas kernels, finish(): pl.pallas_call(finish_kernel, grid=(NA,), out_shape=jax.ShapeDtypeStruct(...  40 us

profile of v2, /device:TPU:32, one launch (start us, length us, event | category | flops | bytes accessed | tf_op | source)
XLA Modules:
  0.0 207.7 jit_solution(1161013084603740536)
XLA Ops:
  0.0 0.6 pad_add_fusion.pos
  0.6 0.7 copy.7
  1.3 0.0 copy-start
  1.3 0.1 compare_reduce_fusion
  1.4 0.1 convert_reduce_fusion
  1.5 0.1 broadcast_in_dim.13
  1.6 1.1 reduce-precision_select_fusion
  2.7 0.8 pad_maximum_fusion.r_0_
  3.4 164.2 %shard_map.28 = (f32[8,5,136,128]{3,2,1,0:T(8,128)}, f32[4,8,5,136,128]{4,3,2,1,0:T(8,128)}, bf16[512,512]{1,0:T(8,128)(2,1)}, bf16[512,512]{1,0:T(8,128)(2,1)},...) custom-call(f32[5,136,128]{2,1,0:T(8,128)} %pad_maximum_fusion.r_0_), custom_call_target="tpu_custom_call" | custom-call | tf_op jit(solution)/shard_map/pallas_call | solution.py:437
  167.7 0.0 copy-done
  167.7 40.0 %shard_map.29 = f32[5,20,128,128]{3,2,1,0:T(8,128)} custom-call(s32[3]{0:T(128)} %pad_add_fusion.pos, s32[5,20]{1,0:T(8,128)} %bitcast.18, f32[8,5,136,128]{3,2,1,0:T(8,128)} %get-tuple-element.14.left, f32[4,8,5,136,128]{4,3,2,1,0:T(8,128)} %get-tuple-element.15.right, bf16[512,512]{1,0:T(8,128)(2,1)} %get-tuple-element.16.w0h, ...), custom_call_target="tpu_custom_call" | custom-call | tf_op jit(solution)/shard_map/pallas_call | solution.py:522
Async XLA Ops:
  1.3 166.4 %copy-start = (s32[5,1,20,1]{2,0,1,3:T(8,128)}, s32[5,1,20,1]{2,0,1,3:T(8,128)S(1)}, u32[]{:S(2)}) copy-start(s32[5,1,20,1]{2,0,1,3:T(8,128)S(1)} %copy.7) | copy-start | bytes 1204

commit v3 on v2

--- a/solution.py
+++ b/solution.py
@@ -30,31 +30,45 @@
 def mm3(a, b, dims):
     return mm(a[0], b[0], dims) + (mm(a[0], b[1], dims) + mm(a[1], b[0], dims))
 
+HALF = PT * 128 // 2
+
+def triple(v, axis):
+    h, l = halves(v)
+    return jnp.concatenate([h, h, l], axis=axis)
+
+def keep_factor(w, wa, wb):
+    h, l = halves(w)
+    wa[...] = jnp.concatenate([h[:HALF, :HALF], l[:HALF, :HALF], h[:HALF, :HALF]], axis=1)
+    wb[...] = jnp.concatenate([h[HALF:], l[HALF:], h[HALF:]], axis=1)
+
+def solve_rows(raw, wa, wb):
+    top = mm(triple(raw[:, :HALF], 1), wa[...], NT)
+    return jnp.concatenate([top, mm(triple(raw, 1), wb[...], NT)], axis=1)
+
 def small_inverse(block):
     lanes = block.shape[1]
-    groups = []
-    for g in range(SUB // 8):
-        low = 8 * g
-        groups.append([jnp.broadcast_to(block[low:, low + e:low + e + 1], (SUB - low, lanes)) for e in range(8)])
+    cols = []
+    for k in range(SUB):
+        low = 8 * (k // 8)
+        cols.append(jnp.broadcast_to(block[low:, k:k + 1], (SUB - low, lanes)))
     row = lax.broadcasted_iota(jnp.int32, (SUB, lanes), 0)
     lane = lax.broadcasted_iota(jnp.int32, (SUB, lanes), 1)
     right = (row == lane).astype(F32)
     done = []
-    cols = [jnp.stack(g, axis=0) for g in groups]
-    for g in range(SUB // 8):
-        for e in range(8):
-            own = cols[g][0]
-            scale = lax.rsqrt(own[e:e + 1])
-            factor = own * scale
-            solved = right[e:e + 1] * scale
-            done.append(solved)
-            right = right - factor * solved
-            if e < 7:
-                cols[g] = cols[g][1:] - factor[None] * factor[e + 1:8][:, None]
-            for h in range(g + 1, SUB // 8):
-                off = 8 * (h - g)
-                cols[h] = cols[h] - factor[off:][None] * factor[off:off + 8][:, None]
-        right = right[8:]
+    for k in range(SUB):
+        low = 8 * (k // 8)
+        own = cols[k]
+        scale = lax.rsqrt(own[k - low:k - low + 1, :])
+        factor = own * scale
+        solved = right[k - low:k - low + 1, :] * scale
+        done.append(solved)
+        if k == SUB - 1:
+            break
+        nxt = 8 * ((k + 1) // 8)
+        for m in range(k + 1, SUB):
+            base = 8 * (m // 8)
+            cols[m] = cols[m] - factor[base - low:, :] * factor[m - low:m - low + 1, :]
+        right = right[nxt - low:, :] - factor[nxt - low:, :] * solved
     return jnp.concatenate(done, axis=0)
 
 def factor_unit(kb, s, a_ref, u_ref, w_ref, t_ref):
@@ -70,9 +84,9 @@
 
         @pl.when(kb > 0)
         def _():
-            left = u_ref[:, here]
-            t_ref[:, :n] -= mm6(left, u_ref[...], TN)
-            t_ref[:, n:] -= mm6(left, w_ref[...], TN)
+            left = halves(u_ref[:, here])
+            t_ref[:, :n] -= mm3(left, halves(u_ref[...]), TN)
+            t_ref[:, n:] -= mm3(left, halves(w_ref[...]), TN)
 
     rows = pl.ds(pl.multiple_of(s * SUB, SUB), SUB)
     out = pl.ds(pl.multiple_of(kb * 128 + s * SUB, SUB), SUB)
@@ -83,7 +97,8 @@
     u_ref[out, :] = jnp.where(lane >= row, both[:, :n], 0.0)
     w_ref[out, :] = jnp.where(lane <= row, both[:, n:], 0.0)
     left = u_ref[out, here]
-    t_ref[...] -= mm6(left, both, TN)
+    hl, hb = halves(left), halves(both)
+    t_ref[...] -= mm(jnp.concatenate([hl[0], hl[0], hl[1]], axis=0), jnp.concatenate([hb[0], hb[1], hb[0]], axis=0), TN)
 
 def tile_of(lead, i, t):
     return lead[t, i, 8:, :]
@@ -117,18 +132,21 @@
     u[...] = jnp.zeros_like(u)
     w[...] = jnp.zeros_like(w)
 
-def chain_turn(z, q, lead, w0h, w0l, p0h, p0l, edge, a, u, w):
+def chain_turn(z, q, lead, w0a, w0b, p0h, p0x, edge, a, u, w):
     edge_tile(z, q, 0, edge, u)
-    w0h[...], w0l[...] = halves(w[...])
+    keep_factor(w[...], w0a, w0b)
+    wide = PT * 128
     for i in range(PT):
         rows = slice(i * 128, (i + 1) * 128)
         raw = jnp.concatenate([tile_of(lead, PT + i, k) for k in range(PT)], axis=1)
-        p0h[rows], p0l[rows] = halves(mm3(halves(raw), (w0h[...], w0l[...]), NT))
+        high, low = halves(solve_rows(raw, w0a, w0b))
+        p0h[rows] = high
+        p0x[rows, :wide], p0x[rows, wide:] = low, high
 
     def updated(i, k):
         hi = slice(i * 128, (i + 1) * 128), slice(k * 128, (k + 1) * 128)
         coarse = mm(p0h[hi[0]], p0h[hi[1]], NT)
-        extra = mm(p0h[hi[0]], p0l[hi[1]], NT) + mm(p0l[hi[0]], p0h[hi[1]], NT)
+        extra = mm(p0h[hi[0]], p0x[hi[1], :wide], NT) + mm(p0x[hi[0], :wide], p0h[hi[1]], NT)
         marked = lead[PT + k, PT + i, 0:1, :] > 0.5
         return tile_of(lead, PT + i, PT + k) - coarse - jnp.where(marked, 0.0, extra)
 
@@ -136,9 +154,9 @@
     u[...] = jnp.zeros_like(u)
     w[...] = jnp.zeros_like(w)
 
-def chain_close(z, q, w1h, w1l, edge, u, w):
+def chain_close(z, q, w1a, w1b, edge, u, w):
     edge_tile(z, q, PT, edge, u)
-    w1h[...], w1l[...] = halves(w[...])
+    keep_factor(w[...], w1a, w1b)
 
 UNITS = 2 * PT * 128 // SUB
 
@@ -158,7 +176,7 @@
 OPEN = 3
 PER = 2
 
-def move_kernel(with_chain, pay_ref, left, right, lead, w0h, w0l, p0h, p0l, w1h, w1l, edge,
+def move_kernel(with_chain, pay_ref, left, right, lead, w0a, w0b, p0h, p0x, w1a, w1b, edge,
                 a_ref, u_ref, w_ref, t_ref, ls, lr, zs, xs, rs, rr, qs, qr, gs, gr, hs, hr):
     x, z, y, c = (lax.axis_index(n) for n in ("x", "z", "y", "c"))
     q = 2 * y + c
@@ -261,6 +279,10 @@
         tip(z, 6, {"z": zm}).start()
 
     for h in range(1, 5):
+        if h == 2:
+            sides.pass_on()
+        if h == 4:
+            sides.share()
         row = lax.rem(z - h + NZ, NZ)
         tip(row, 0, other).wait_recv()
         if h < 4:
@@ -271,9 +293,7 @@
                 tip(row, 6 + h, {"z": zm}).start()
 
     upper.open()
-    sides.pass_on()
     lower.open()
-    sides.share()
     sides.close()
     left[pl.ds(q, 1)] = pay_ref[...][None]
 
@@ -379,12 +399,12 @@
         for i in range(PER):
             unit = PER * (m - OPEN) + i
             inside(unit, 0, UNITS, lambda: chain_unit(
-                unit, jnp.where(x == 0, z, 4 * PT), q, lead, (w0h, w0l, p0h, p0l), edge, a_ref, u_ref, w_ref, t_ref))
+                unit, jnp.where(x == 0, z, 4 * PT), q, lead, (w0a, w0b, p0h, p0x), edge, a_ref, u_ref, w_ref, t_ref))
         return carry
 
     steps = max(4 * NS + 7 * ZL + FL, OPEN + UNITS // PER)
     lax.fori_loop(0, steps, step, 0)
-    chain_close(jnp.where(x == 0, z, 4 * PT), q, w1h, w1l, edge, u_ref, w_ref)
+    chain_close(jnp.where(x == 0, z, 4 * PT), q, w1a, w1b, edge, u_ref, w_ref)
 
     @pl.when(z == q)
     def _():
@@ -432,11 +452,12 @@
     V = pl.BlockSpec(memory_space=pltpu.VMEM)
     D = pltpu.SemaphoreType.DMA
     wide = PT * 128
-    half = jax.ShapeDtypeStruct((wide, wide), BF16)
+    half = lambda *s: jax.ShapeDtypeStruct(s, BF16)
     shape = lambda *s: jax.ShapeDtypeStruct(s, F32)
     return pl.pallas_call(
         lambda *r: move_kernel(True, *r[:3], r[10], *r[3:10], *r[11:]),
-        out_shape=[shape(NTC, NA, PR, 128), shape(NX, NTC, NA, PR, 128)] + [half] * 6 + [shape(128, 128)],
+        out_shape=[shape(NTC, NA, PR, 128), shape(NX, NTC, NA, PR, 128)] + [half(HALF, 3 * HALF), half(HALF, 3 * wide), half(wide, wide), half(wide, 2 * wide), half(HALF, 3 * HALF),
+                      half(HALF, 3 * wide)] + [shape(128, 128)],
         in_specs=[V], out_specs=[V] * 9,
         scratch_shapes=[pltpu.VMEM((NTC, NTC, PR, 128), F32)] + [pltpu.VMEM((wide, wide), F32)] * 3
         + [pltpu.VMEM((128, 2 * wide), F32)]
@@ -445,18 +466,17 @@
         compiler_params=pltpu.CompilerParams(collective_id=0, has_side_effects=True, vmem_limit_bytes=60 * 2**20),
     )(pay)
 
-def finish_kernel(pos, marks, left, right, w0h, w0l, p0h, p0l, w1h, w1l, edge, work, out, lh, ll, rh, rl):
+def finish_kernel(pos, marks, left, right, w0a, w0b, p0h, p0x, w1a, w1b, edge, work, out, own, opp):
     r, q = pos[2], pos[1]
     group = pl.program_id(0)
     wide = PT * 128
 
-    def solve(read, count, high, low):
+    def solve(read, count):
         raw = jnp.concatenate(
             [jnp.concatenate([read(m, k)[8:] for k in range(PT)], axis=1) for m in range(count)], axis=0)
-        first = halves(mm3(halves(raw), (w0h[...], w0l[...]), NT))
-        high[:, :wide], low[:, :wide] = first
-        coarse = mm(first[0], p0h[...], NT)
-        extra = mm(first[0], p0l[...], NT) + mm(first[1], p0h[...], NT)
+        high, low = halves(solve_rows(raw, w0a, w0b))
+        coarse = mm(high, p0h[...], NT)
+        extra = mm(jnp.concatenate([high, low], axis=1), p0x[...], NT)
         parts = []
         for m in range(count):
             rows = slice(m * 128, (m + 1) * 128)
@@ -466,49 +486,48 @@
                 piece = read(m, PT + k)
                 row.append(piece[8:] - coarse[rows, lanes] - jnp.where(piece[0:1] > 0.5, 0.0, extra[rows, lanes]))
             parts.append(jnp.concatenate(row, axis=1))
-        second = halves(mm3(halves(jnp.concatenate(parts, axis=0)), (w1h[...], w1l[...]), NT))
-        high[:, wide:], low[:, wide:] = second
+        return (high, low), halves(solve_rows(jnp.concatenate(parts, axis=0), w1a, w1b))
 
     @pl.when(group == 0)
     def _():
-        solve(lambda m, k: left[k, m], NA, lh, ll)
-
-    solve(lambda m, k: right[m, k, 0], NX, rh, rl)
-
-    def one_row(a, carry):
-        i = a * 32 + r
-
-        @pl.when(a >= group)
-        def _():
-            rows = pl.ds(pl.multiple_of(a * 128, 128), 128)
-            own_h, own_l = lh[rows, :], ll[rows, :]
-            coarse = mm(own_h, rh[...], NT)
-            extra = mm(own_h, rl[...], NT) + mm(own_l, rh[...], NT)
+        first, second = solve(lambda m, k: left[k, m], NA)
+        for i, v in enumerate((first[0], second[0], first[1], second[1])):
+            own[:, i * wide:(i + 1) * wide] = v
+
+    first, second = solve(lambda m, k: right[m, k, 0], NX)
+    for i, v in enumerate((first[1], second[1], first[0], second[0])):
+        opp[:, i * wide:(i + 1) * wide] = v
+
+    def rows_from(g):
+        coarse = mm(own[g * 128:, :2 * wide], opp[:, 2 * wide:], NT)
+        extra = mm(own[g * 128:, :], opp[...], NT)
+        for a in range(NA):
+            if a < g:
+                out[a] = jnp.zeros((NX, 128, 128), F32)
+                continue
+            i = a * 32 + r
+            rows = slice((a - g) * 128, (a - g + 1) * 128)
             for m in range(NX):
                 lanes = slice(m * 128, (m + 1) * 128)
-                j = group * 32 + m * 8 + q
-                mark = marks[a, group * NX + m]
+                j = g * 32 + m * 8 + q
+                mark = marks[a, g * NX + m]
                 tile = work[a, m]
-                exact = tile - (coarse[:, lanes] + extra[:, lanes])
-                rough = tile.astype(BF16).astype(F32) - coarse[:, lanes]
+                exact = tile - (coarse[rows, lanes] + extra[rows, lanes])
+                rough = tile.astype(BF16).astype(F32) - coarse[rows, lanes]
                 rough = rough.astype(BF16).astype(F32)
                 value = jnp.where(mark == 1, rough, exact)
                 out[a, m] = jnp.where(i >= j, value, 0.0)
 
-        @pl.when(a < group)
-        def _():
-            out[a] = jnp.zeros((NX, 128, 128), F32)
-        return carry
-
-    lax.fori_loop(0, NA, one_row, 0)
+    for g in range(NA):
+        pl.when(group == g)(lambda g=g: rows_from(g))
 
     @pl.when(group == 0)
     def _():
-        lanes = pl.ds(pl.multiple_of(q * 128, 128), 128)
         for a in range(NA):
             i = a * 32 + r
             rows = slice(a * 128, (a + 1) * 128)
-            value = lh[rows, lanes].astype(F32) + ll[rows, lanes].astype(F32)
+            value = (own[rows, pl.ds(pl.multiple_of(q * 128, 128), 128)].astype(F32)
+                     + own[rows, pl.ds(pl.multiple_of(2 * wide + q * 128, 128), 128)].astype(F32))
             if a == 0:
                 value = jnp.where((i < 2 * PT) & (i // PT == q // PT), edge[...], value)
             value = jnp.where(marks[a, 0] == 1, value.astype(BF16).astype(F32), value)
@@ -526,7 +545,7 @@
         in_specs=[S, S, whole(left.shape), pl.BlockSpec((NX, NTC, 1, PR, 128), lambda g: (0, 0, g, 0, 0))]
         + [whole(v.shape) for v in parts] + [tiles],
         out_specs=tiles,
-        scratch_shapes=[pltpu.VMEM((NA * 128, 2 * wide), BF16)] * 2 + [pltpu.VMEM((NX * 128, 2 * wide), BF16)] * 2,
+        scratch_shapes=[pltpu.VMEM((NA * 128, 4 * wide), BF16), pltpu.VMEM((NX * 128, 4 * wide), BF16)],
         compiler_params=pltpu.CompilerParams(vmem_limit_bytes=60 * 2**20, dimension_semantics=("arbitrary",)),
     )(pos, marks, left, right, *parts, work)
 

time: 210 us -> 187 us (0.89)
  Pallas kernels: 204 us -> 182 us
    pallas_call x1, Pallas kernels: 164 us -> 149 us  [move(): pl.pallas_call(lambda *r: move_kernel(True, *r[:3], r[10], *r[3:10], *r[1...]
    pallas_call x1, Pallas kernels: 40 us -> 32.4 us  [finish(): pl.pallas_call(finish_kernel, grid=(NA,), out_shape=jax.ShapeDtypeStruct(...]
where the time goes in v3:
time: 187 us; the launch traced here: 185 us
  Pallas kernels  182 us (97%)
  other arithmetic  2.71 us (1%)
    pallas_call x1, Pallas kernels, move(): pl.pallas_call(lambda *r: move_kernel(True, *r[:3], r[10], *r[3:10], *r[1...  149 us
    pallas_call x1, Pallas kernels, finish(): pl.pallas_call(finish_kernel, grid=(NA,), out_shape=jax.ShapeDtypeStruct(...  32.4 us

profile of v3, /device:TPU:32, one launch (start us, length us, event | category | flops | bytes accessed | tf_op | source)
XLA Modules:
  0.0 185.1 jit_solution(7739434081239427436)
XLA Ops:
  0.0 0.7 pad_add_fusion.pos
  0.7 0.7 copy.7
  1.3 0.0 copy-start
  1.3 0.1 compare_reduce_fusion
  1.5 0.1 convert_reduce_fusion
  1.6 0.1 broadcast_in_dim.13
  1.6 1.1 reduce-precision_select_fusion
  2.7 0.8 pad_maximum_fusion.r_0_
  3.5 149.2 %shard_map.28 = (f32[8,5,136,128]{3,2,1,0:T(8,128)}, f32[4,8,5,136,128]{4,3,2,1,0:T(8,128)}, bf16[256,768]{1,0:T(8,128)(2,1)}, bf16[256,1536]{1,0:T(8,128)(2,1)}...) custom-call(f32[5,136,128]{2,1,0:T(8,128)} %pad_maximum_fusion.r_0_), custom_call_target="tpu_custom_call" | custom-call | tf_op jit(solution)/shard_map/pallas_call | solution.py:457
  152.7 0.0 copy-done
  152.7 32.4 %shard_map.29 = f32[5,20,128,128]{3,2,1,0:T(8,128)} custom-call(s32[3]{0:T(128)} %pad_add_fusion.pos, s32[5,20]{1,0:T(8,128)} %bitcast.18, f32[8,5,136,128]{3,2,1,0:T(8,128)} %get-tuple-element.14.left, f32[4,8,5,136,128]{4,3,2,1,0:T(8,128)} %get-tuple-element.15.right, bf16[256,768]{1,0:T(8,128)(2,1)} %get-tuple-element.16.w0a, ...), custom_call_target="tpu_custom_call" | custom-call | tf_op jit(solution)/shard_map/pallas_call | solution.py:541
Async XLA Ops:
  1.3 151.4 %copy-start = (s32[5,1,20,1]{2,0,1,3:T(8,128)}, s32[5,1,20,1]{2,0,1,3:T(8,128)S(1)}, u32[]{:S(2)}) copy-start(s32[5,1,20,1]{2,0,1,3:T(8,128)S(1)} %copy.7) | copy-start | bytes 1204

commit v4 on v3

--- a/solution.py
+++ b/solution.py
@@ -171,13 +171,14 @@
 
 NX, NZ, NY, NA, NTC = 4, 8, 4, 5, 8
 PR = 136
-ZL, RL, FL, OFF = 1, 2, 4, 1
-NS = 3
-OPEN = 3
+ZL, RL, FL, OFF = 1, 2, 4, 4
+NS = 4
+OPEN = 7
+EARLY = 2
 PER = 2
 
 def move_kernel(with_chain, pay_ref, left, right, lead, w0a, w0b, p0h, p0x, w1a, w1b, edge,
-                a_ref, u_ref, w_ref, t_ref, ls, lr, zs, xs, rs, rr, qs, qr, gs, gr, hs, hr):
+                a_ref, u_ref, w_ref, t_ref, ls, lr, zs, xs, rs, rr, qs, qr, gs, gr, hs, hr, es, er):
     x, z, y, c = (lax.axis_index(n) for n in ("x", "z", "y", "c"))
     q = 2 * y + c
     xp, xm, xfar = lax.rem(x + 1, NX), lax.rem(x + NX - 1, NX), lax.rem(x + 2, NX)
@@ -250,11 +251,14 @@
                 self.on(k, go)
             self.on(2 * yo + c, lambda: sent(2 * yo + c, 2))
 
-    sides = Gather(pay_ref, lambda k: left.at[k], ls, lr, NTC)
+    first, rest = pl.ds(0, EARLY), pl.ds(EARLY, NA - EARLY)
+    sides = Gather(pay_ref.at[first], lambda k: left.at[k, first], ls, lr, NTC)
+    later = Gather(pay_ref.at[rest], lambda k: left.at[k, rest], es, er, NTC)
     upper = Gather(lead.at[q, pl.ds(0, PT)], lambda k: lead.at[k, pl.ds(0, PT)], gs, gr, PT)
     lower = Gather(lead.at[q, pl.ds(PT, PT)], lambda k: lead.at[k, pl.ds(PT, PT)], hs, hr, NTC)
 
     sides.open()
+    later.open()
 
     mine = pay_ref.at[0]
     def tip(row, send, where, src=None):
@@ -278,11 +282,7 @@
         tip(z, 2, {"z": zp}).start()
         tip(z, 6, {"z": zm}).start()
 
-    for h in range(1, 5):
-        if h == 2:
-            sides.pass_on()
-        if h == 4:
-            sides.share()
+    def ring(h):
         row = lax.rem(z - h + NZ, NZ)
         tip(row, 0, other).wait_recv()
         if h < 4:
@@ -292,8 +292,8 @@
             if h < 3:
                 tip(row, 6 + h, {"z": zm}).start()
 
-    upper.open()
-    lower.open()
+    sides.pass_on()
+    sides.share()
     sides.close()
     left[pl.ds(q, 1)] = pay_ref[...][None]
 
@@ -374,20 +374,29 @@
         for par in range(2):
             n = m - zd[par] * ZL
             inside(n, 0, 4 * NS, lambda: near(par, n))
-            @pl.when((zd[par] == 0) & (n < far // 2))
-            def _():
-                spread(par, 4 * NS + 2 * n)
-                spread(par, 4 * NS + 2 * n + 1)
+            @pl.when((zd[par] == 0) & (n >= OFF) & (n < far // 2 + OFF))
+            def _():
+                spread(par, 4 * NS + 2 * (n - OFF))
+                spread(par, 4 * NS + 2 * (n - OFF) + 1)
             inside(n - RL, 0, 4 * NS, lambda: relay(par, n - RL))
-            @pl.when((zd[par] == 0) & (n >= RL) & (n < far // 2 + RL))
-            def _():
-                relay(par, 4 * NS + 2 * (n - RL))
-                relay(par, 4 * NS + 2 * (n - RL) + 1)
-            for i in range(3):
-                k = 3 * (n - OFF) + i
+            @pl.when((zd[par] == 0) & (n >= OFF + RL) & (n < far // 2 + OFF + RL))
+            def _():
+                relay(par, 4 * NS + 2 * (n - OFF - RL))
+                relay(par, 4 * NS + 2 * (n - OFF - RL) + 1)
+            for i in range(2):
+                k = 2 * (n - OFF) + i
                 inside(k, 0, NX * far, lambda: stream(par, k))
             inside(n - FL, 0, 4 * NS, lambda: last_landed(par, n - FL))
-        pl.when(m == 1)(upper.pass_on)
+        for h in range(1, 5):
+            pl.when(m == h - 1)(lambda h=h: ring(h))
+        pl.when(m == 1)(later.pass_on)
+        pl.when(m == 2)(later.share)
+        @pl.when(m == 3)
+        def _():
+            later.close()
+            upper.open()
+            lower.open()
+        pl.when(m == OPEN - 2)(upper.pass_on)
         @pl.when(m == OPEN)
         def _():
             upper.share()
@@ -411,6 +420,7 @@
         right[pl.ds(x, 1)] = left[...][None]
 
     sides.drain()
+    later.drain()
     upper.drain()
     lower.drain()
 
@@ -462,7 +472,7 @@
         scratch_shapes=[pltpu.VMEM((NTC, NTC, PR, 128), F32)] + [pltpu.VMEM((wide, wide), F32)] * 3
         + [pltpu.VMEM((128, 2 * wide), F32)]
         + [D((8, 3)), D((8,)), D((4, 8, 5)), D((8, 5, 2)), D((8, 5)), D((4, 8, 5)), D((9,)), D((8,)),
-           D((8, 3)), D((8,)), D((8, 3)), D((8,))],
+           D((8, 3)), D((8,)), D((8, 3)), D((8,)), D((8, 3)), D((8,))],
         compiler_params=pltpu.CompilerParams(collective_id=0, has_side_effects=True, vmem_limit_bytes=60 * 2**20),
     )(pay)
 

time: 187 us -> 176 us (0.941)
  Pallas kernels: 182 us -> 172 us
    pallas_call x1, Pallas kernels: 149 us -> 140 us  [move(): pl.pallas_call(lambda *r: move_kernel(True, *r[:3], r[10], *r[3:10], *r[1...]
where the time goes in v4:
time: 176 us; the launch traced here: 175 us
  Pallas kernels  172 us (98%)
  other arithmetic  2.71 us (2%)
    pallas_call x1, Pallas kernels, move(): pl.pallas_call(lambda *r: move_kernel(True, *r[:3], r[10], *r[3:10], *r[1...  140 us
    pallas_call x1, Pallas kernels, finish(): pl.pallas_call(finish_kernel, grid=(NA,), out_shape=jax.ShapeDtypeStruct(...  32.4 us

profile of v4, /device:TPU:32, one launch (start us, length us, event | category | flops | bytes accessed | tf_op | source)
XLA Modules:
  0.0 175.4 jit_solution(5902880761979422522)
XLA Ops:
  0.0 0.7 pad_add_fusion.pos
  0.7 0.7 copy.7
  1.3 0.0 copy-start
  1.3 0.1 compare_reduce_fusion
  1.5 0.1 convert_reduce_fusion
  1.6 0.1 broadcast_in_dim.13
  1.6 1.1 reduce-precision_select_fusion
  2.7 0.8 pad_maximum_fusion.r_0_
  3.5 139.5 %shard_map.28 = (f32[8,5,136,128]{3,2,1,0:T(8,128)}, f32[4,8,5,136,128]{4,3,2,1,0:T(8,128)}, bf16[256,768]{1,0:T(8,128)(2,1)}, bf16[256,1536]{1,0:T(8,128)(2,1)}...) custom-call(f32[5,136,128]{2,1,0:T(8,128)} %pad_maximum_fusion.r_0_), custom_call_target="tpu_custom_call" | custom-call | tf_op jit(solution)/shard_map/pallas_call | solution.py:467
  143.0 0.0 copy-done
  143.0 32.4 %shard_map.29 = f32[5,20,128,128]{3,2,1,0:T(8,128)} custom-call(s32[3]{0:T(128)} %pad_add_fusion.pos, s32[5,20]{1,0:T(8,128)} %bitcast.18, f32[8,5,136,128]{3,2,1,0:T(8,128)} %get-tuple-element.14.left, f32[4,8,5,136,128]{4,3,2,1,0:T(8,128)} %get-tuple-element.15.right, bf16[256,768]{1,0:T(8,128)(2,1)} %get-tuple-element.16.w0a, ...), custom_call_target="tpu_custom_call" | custom-call | tf_op jit(solution)/shard_map/pallas_call | solution.py:551
Async XLA Ops:
  1.3 141.7 %copy-start = (s32[5,1,20,1]{2,0,1,3:T(8,128)}, s32[5,1,20,1]{2,0,1,3:T(8,128)S(1)}, u32[]{:S(2)}) copy-start(s32[5,1,20,1]{2,0,1,3:T(8,128)S(1)} %copy.7) | copy-start | bytes 1204
